TPU v7x, 256 devices: a whole 4x4x8 slice. The times are simulated.
256 devices in a mesh: mkt: 8 (over x, core), trade: 8 (over y, z_hi), scen: 4 (over z_lo).
Axes of the slice: x: 4, y: 4, z: 8 (z_hi: 2, z_lo: 4; z = z_hi * 4 + z_lo), core: 2. Of those that a mesh axis runs over, the one named last changes fastest.
Arguments:
- quotes: bfloat16 [512, 4096], P('mkt'), may hold values from -6 to 6
- kernel: bfloat16 [512, 128, 128], P(('trade', 'scen')), may hold values from -0.5 to 0.5
- trade_block: int32 [16384], P('trade'), may hold values from 0 to 511
- trade_embed: bfloat16 [16384, 256], P('trade'), may hold values from -6 to 6
- position: float32 [16384], P('trade'), may hold values from -0.046875 to 0.046875
- scen_rank: int32 [512], P(('mkt', 'scen')), may hold values from 0 to 511, each once
- w_in: bfloat16 [128, 256], replicated, may hold values from -0.5 to 0.5
- w_mid: bfloat16 [256, 256], replicated, may hold values from -0.375 to 0.375
- b_mid: float32 [256], replicated, may hold values from -6 to 6
- w_out: bfloat16 [256], replicated, may hold values from -0.375 to 0.375
Outputs:
- book_pnl: float32 [512], P(('mkt', 'scen'))
- marginal: float32 [16384], P('trade')
- shortfall: float32 [], replicated
Inputs may be any that keep to these rules, and one draw needn't show every extreme that they name: scen_rank holds each rank of 0 to 511 once.
All inputs are finite; a program needn't handle non-finite values.
Results may differ from a plain program's by a relative error of at most 0.014.
The roundings to bfloat16 on the way count: a program that leaves them out, or rounds other values in their place, can miss the bound.
Values may be sent and summed in bfloat16 or wider, within the bound.
A program may use at most 64 MiB of HBM per device.

v0:
```python
import jax
import jax.numpy as jnp
from jax import lax
from jax.sharding import PartitionSpec as P

SEG = 128
WIN = 128
QSTEP = 8


def copy_for_each(x, axis):
    size = lax.axis_size(axis)
    return lax.all_to_all(jnp.broadcast_to(x[None], (size, *x.shape)), axis, 0, 0, tiled=True)


def laid_out(blocks, dim):
    blocks = jnp.moveaxis(blocks, 0, dim)
    shape = blocks.shape
    return blocks.reshape(*shape[:dim], shape[dim] * shape[dim + 1], *shape[dim + 2 :])


def gather_directly(x, axis, dim):
    blocks = copy_for_each(x, axis)
    return laid_out(blocks, dim)


def of_everyone(x, axis):
    return copy_for_each(x, axis).sum(axis=0)


def in_one(arrays, axis):
    ends = [0]
    for a in arrays:
        ends.append(ends[-1] + a.size)
    subtotal = of_everyone(jnp.concatenate([a.ravel() for a in arrays]), axis)
    return tuple((subtotal[b:e].reshape(a.shape) for a, b, e in zip(arrays, ends, ends[1:])))


def local(quotes, kernel, trade_block, trade_embed, position, scen_rank, w_in, w_mid, b_mid, w_out):
    local_count = kernel.shape[0]
    quote_count = quotes.shape[1]
    row_count = quotes.shape[0]
    first_block = lax.axis_index(("trade", "scen")) * local_count

    def cut_window(local_block):
        block_index = first_block + local_block
        window_start = jnp.clip(QSTEP * block_index - (WIN - QSTEP) // 2, 0, quote_count - WIN)
        return lax.dynamic_slice_in_dim(quotes, window_start, WIN, 1)

    windows = jax.vmap(cut_window)(jnp.arange(local_count, dtype=jnp.int32))
    built_state = jnp.einsum("jrw,jws->jrs", windows, kernel, preferred_element_type=jnp.float32)
    built_state = built_state.astype(jnp.bfloat16).reshape(local_count, row_count * SEG)
    scen_count = scen_rank.shape[0]
    quarter = lax.all_to_all(built_state, "scen", split_axis=1, concat_axis=0, tiled=True)
    table = gather_directly(quarter, "trade", 0)
    trade_rows_all = table[trade_block]
    embed_float = trade_embed.astype(jnp.float32)

    def price(scen_index):
        trade_rows = lax.dynamic_slice_in_dim(trade_rows_all, scen_index * SEG, SEG, 1)
        hidden_one = jax.nn.silu(
            jnp.dot(trade_rows, w_in, preferred_element_type=jnp.float32) + embed_float
        ).astype(jnp.bfloat16)
        hidden_two = jax.nn.silu(
            jnp.dot(hidden_one, w_mid, preferred_element_type=jnp.float32) + b_mid
        ).astype(jnp.bfloat16)
        return jnp.dot(hidden_two, w_out, preferred_element_type=jnp.float32)

    values = lax.map(price, jnp.arange(scen_count, dtype=jnp.int32))
    scen_total = scen_count * lax.axis_size("mkt") * lax.axis_size("scen")
    decay_span = scen_total // 20
    weight_sum = jnp.sum(jnp.exp(-jnp.arange(scen_total, dtype=jnp.float32) / decay_span))
    weights = jnp.exp(-scen_rank.astype(jnp.float32) / decay_span) / weight_sum
    pnl_part = jnp.dot(values, position, precision=lax.Precision.HIGHEST)
    marginal = of_everyone(
        -jnp.dot(weights, values, precision=lax.Precision.HIGHEST), ("mkt", "scen")
    )
    own_share = jnp.dot(position, marginal, precision=lax.Precision.HIGHEST)
    book_pnl, shortfall = in_one((pnl_part, own_share), "trade")
    return (book_pnl, marginal, shortfall)


def solution(mesh):
    placed = (
        P("mkt", None),
        P(("trade", "scen"), None, None),
        P("trade"),
        P("trade", None),
        P("trade"),
        P(("mkt", "scen")),
        P(),
        P(),
        P(),
        P(),
    )
    return jax.shard_map(
        local,
        mesh=mesh,
        in_specs=placed,
        out_specs=(P(("mkt", "scen")), P("trade"), P()),
        check_vma=False,
    )
```

profile of v0, /device:TPU:1, one launch (start us, length us, event | category | flops | bytes accessed | tf_op | source)
XLA Modules:
  0.0 232.0 jit_solution(4308197242800511816)
XLA Ops:
  0.7 33.3 %while.12 = (s32[]{:T(128)}, bf16[64,4096]{1,0:T(8,128)(2,1)}, s32[16,2]{0,1:T(2,128)S(1)}, bf16[16,64,128]{2,1,0:T(8,128)(2,1)S(1)}, s32[]{:T(128)}) while((s32[]{:T(128)}, bf16[64,4096]{1,0:T(8,128)(2,1)}, s32[16,2]{0,1:T(2,128)S(1)}, bf16[16,64,128]{2,1,0:T(8,128)(2,1)S(1)}, s32[]{:T(128)}) %tuple.33), condition=%wide.while_cond, body=%wide.while_body.sunk | while | flops 2 | bytes 32865 | solution.py:48
  34.5 13.1 %all_to_all.33 = bf16[16,4,2048]{2,0,1:T(8,128)(2,1)S(1)} all-to-all(bf16[16,4,2048]{2,0,1:T(8,128)(2,1)S(1)} %copy.15), channel_id=1, replica_groups=mesh['mkt'=8,'trade'=8,'scen'=4] {'scen'}, dimensions={1} | all-to-all | bytes 524288 | tf_op jit(solution)/shard_map/all_to_all | solution.py:54
  49.2 8.1 %all-to-all-start.1 = ((bf16[8,64,2048]{2,1,0:T(8,128)(2,1)}), bf16[8,64,2048]{2,1,0:T(8,128)(2,1)S(1)}, u32[]{:S(2)}, u32[]{:S(2)}) async-start(bf16[8,64,2048]{2,1,0:T(8,128)(2,1)} %broadcast_in_dim.34), calls=%async_computation.1 | async-start | bytes 4194304 | tf_op jit(solution)/shard_map/all_to_all | solution.py:13
  57.3 2.7 %convert_element_type.16 = f32[2048,256]{1,0:T(8,128)} convert(bf16[2048,256]{1,0:T(8,128)(2,1)} %param.15) | non-fusion elementwise | flops 524288 | bytes 3145728 | tf_op jit(solution)/shard_map/convert_element_type | solution.py:57
  60.7 27.9 %all-to-all-done.1 = bf16[8,64,2048]{2,1,0:T(8,128)(2,1)S(1)} async-done(((bf16[8,64,2048]{2,1,0:T(8,128)(2,1)}), bf16[8,64,2048]{2,1,0:T(8,128)(2,1)S(1)}, u32[]{:S(2)}, u32[]{:S(2)}) %all-to-all-start.1) | async-done | bytes 2097184 | tf_op jit(solution)/shard_map/all_to_all | solution.py:13
  88.6 11.0 %gather_fusion = bf16[2048,2048]{1,0:T(8,128)(2,1)} fusion(bf16[512,2048]{1,0:T(8,128)(2,1)S(1)} %bitcast.43, s32[2048]{0:T(1024)S(1)} %fusion.6), kind=kCustom, calls=%fused_computation | custom fusion | bytes 16785408 | tf_op jit(solution)/shard_map/gather | solution.py:56
  99.6 76.4 %while.11 = (s32[]{:T(128)}, f32[16,2048]{1,0:T(8,128)S(1)}, s32[16]{0:T(128)S(1)}, bf16[2048,2048]{1,0:T(8,128)(2,1)}, bf16[128,256]{1,0:T(8,128)(2,1)S(1)}, /*...) while((s32[]{:T(128)}, f32[16,2048]{1,0:T(8,128)S(1)}, ...), condition=%wide.region_1.2_spmd, body=%wide.region_0.1_spmd.sunk | while | flops 409993216 | bytes 4942527 | solution.py:69
  105.6 2.5 %multiply_convert_fusion.3 = bf16[2048,256]{1,0:T(8,128)(2,1)S(1)} fusion(f32[2048,256]{1,0:T(8,128)} %get-tuple-element.211, bf16[128,256]{1,0:T(8,128)(2,1)S(1)} %get-tuple-element.210, bf16[2048,2048]{1,0:T(8,128)(2,1)} %get-tuple-element.209, s32[]{:T(128)S(6)} %select_n.23), kind=kOutput, calls=%fused_computation.4.clone.1 | convolution fusion | flops 137363456 | bytes 3735556 | tf_op jit(solution)/shard_map/while/body/eval_jaxpr/dot_general | solution.py:62
  110.4 2.5 %multiply_convert_fusion.3 = bf16[2048,256]{1,0:T(8,128)(2,1)S(1)} fusion(f32[2048,256]{1,0:T(8,128)} %get-tuple-element.211, bf16[128,256]{1,0:T(8,128)(2,1)S(1)} %get-tuple-element.210, bf16[2048,2048]{1,0:T(8,128)(2,1)} %get-tuple-element.209, s32[]{:T(128)S(6)} %select_n.23), kind=kOutput, calls=%fused_computation.4.clone.1 | convolution fusion | flops 137363456 | bytes 3735556 | tf_op jit(solution)/shard_map/while/body/eval_jaxpr/dot_general | solution.py:62
  115.2 2.5 %multiply_convert_fusion.3 = bf16[2048,256]{1,0:T(8,128)(2,1)S(1)} fusion(f32[2048,256]{1,0:T(8,128)} %get-tuple-element.211, bf16[128,256]{1,0:T(8,128)(2,1)S(1)} %get-tuple-element.210, bf16[2048,2048]{1,0:T(8,128)(2,1)} %get-tuple-element.209, s32[]{:T(128)S(6)} %select_n.23), kind=kOutput, calls=%fused_computation.4.clone.1 | convolution fusion | flops 137363456 | bytes 3735556 | tf_op jit(solution)/shard_map/while/body/eval_jaxpr/dot_general | solution.py:62
  119.9 2.5 %multiply_convert_fusion.3 = bf16[2048,256]{1,0:T(8,128)(2,1)S(1)} fusion(f32[2048,256]{1,0:T(8,128)} %get-tuple-element.211, bf16[128,256]{1,0:T(8,128)(2,1)S(1)} %get-tuple-element.210, bf16[2048,2048]{1,0:T(8,128)(2,1)} %get-tuple-element.209, s32[]{:T(128)S(6)} %select_n.23), kind=kOutput, calls=%fused_computation.4.clone.1 | convolution fusion | flops 137363456 | bytes 3735556 | tf_op jit(solution)/shard_map/while/body/eval_jaxpr/dot_general | solution.py:62
  124.7 2.5 %multiply_convert_fusion.3 = bf16[2048,256]{1,0:T(8,128)(2,1)S(1)} fusion(f32[2048,256]{1,0:T(8,128)} %get-tuple-element.211, bf16[128,256]{1,0:T(8,128)(2,1)S(1)} %get-tuple-element.210, bf16[2048,2048]{1,0:T(8,128)(2,1)} %get-tuple-element.209, s32[]{:T(128)S(6)} %select_n.23), kind=kOutput, calls=%fused_computation.4.clone.1 | convolution fusion | flops 137363456 | bytes 3735556 | tf_op jit(solution)/shard_map/while/body/eval_jaxpr/dot_general | solution.py:62
  129.5 2.5 %multiply_convert_fusion.3 = bf16[2048,256]{1,0:T(8,128)(2,1)S(1)} fusion(f32[2048,256]{1,0:T(8,128)} %get-tuple-element.211, bf16[128,256]{1,0:T(8,128)(2,1)S(1)} %get-tuple-element.210, bf16[2048,2048]{1,0:T(8,128)(2,1)} %get-tuple-element.209, s32[]{:T(128)S(6)} %select_n.23), kind=kOutput, calls=%fused_computation.4.clone.1 | convolution fusion | flops 137363456 | bytes 3735556 | tf_op jit(solution)/shard_map/while/body/eval_jaxpr/dot_general | solution.py:62
  134.3 2.5 %multiply_convert_fusion.3 = bf16[2048,256]{1,0:T(8,128)(2,1)S(1)} fusion(f32[2048,256]{1,0:T(8,128)} %get-tuple-element.211, bf16[128,256]{1,0:T(8,128)(2,1)S(1)} %get-tuple-element.210, bf16[2048,2048]{1,0:T(8,128)(2,1)} %get-tuple-element.209, s32[]{:T(128)S(6)} %select_n.23), kind=kOutput, calls=%fused_computation.4.clone.1 | convolution fusion | flops 137363456 | bytes 3735556 | tf_op jit(solution)/shard_map/while/body/eval_jaxpr/dot_general | solution.py:62
  139.0 2.5 %multiply_convert_fusion.3 = bf16[2048,256]{1,0:T(8,128)(2,1)S(1)} fusion(f32[2048,256]{1,0:T(8,128)} %get-tuple-element.211, bf16[128,256]{1,0:T(8,128)(2,1)S(1)} %get-tuple-element.210, bf16[2048,2048]{1,0:T(8,128)(2,1)} %get-tuple-element.209, s32[]{:T(128)S(6)} %select_n.23), kind=kOutput, calls=%fused_computation.4.clone.1 | convolution fusion | flops 137363456 | bytes 3735556 | tf_op jit(solution)/shard_map/while/body/eval_jaxpr/dot_general | solution.py:62
  143.8 2.5 %multiply_convert_fusion.3 = bf16[2048,256]{1,0:T(8,128)(2,1)S(1)} fusion(f32[2048,256]{1,0:T(8,128)} %get-tuple-element.211, bf16[128,256]{1,0:T(8,128)(2,1)S(1)} %get-tuple-element.210, bf16[2048,2048]{1,0:T(8,128)(2,1)} %get-tuple-element.209, s32[]{:T(128)S(6)} %select_n.23), kind=kOutput, calls=%fused_computation.4.clone.1 | convolution fusion | flops 137363456 | bytes 3735556 | tf_op jit(solution)/shard_map/while/body/eval_jaxpr/dot_general | solution.py:62
  148.6 2.5 %multiply_convert_fusion.3 = bf16[2048,256]{1,0:T(8,128)(2,1)S(1)} fusion(f32[2048,256]{1,0:T(8,128)} %get-tuple-element.211, bf16[128,256]{1,0:T(8,128)(2,1)S(1)} %get-tuple-element.210, bf16[2048,2048]{1,0:T(8,128)(2,1)} %get-tuple-element.209, s32[]{:T(128)S(6)} %select_n.23), kind=kOutput, calls=%fused_computation.4.clone.1 | convolution fusion | flops 137363456 | bytes 3735556 | tf_op jit(solution)/shard_map/while/body/eval_jaxpr/dot_general | solution.py:62
  153.4 2.5 %multiply_convert_fusion.3 = bf16[2048,256]{1,0:T(8,128)(2,1)S(1)} fusion(f32[2048,256]{1,0:T(8,128)} %get-tuple-element.211, bf16[128,256]{1,0:T(8,128)(2,1)S(1)} %get-tuple-element.210, bf16[2048,2048]{1,0:T(8,128)(2,1)} %get-tuple-element.209, s32[]{:T(128)S(6)} %select_n.23), kind=kOutput, calls=%fused_computation.4.clone.1 | convolution fusion | flops 137363456 | bytes 3735556 | tf_op jit(solution)/shard_map/while/body/eval_jaxpr/dot_general | solution.py:62
  158.1 2.5 %multiply_convert_fusion.3 = bf16[2048,256]{1,0:T(8,128)(2,1)S(1)} fusion(f32[2048,256]{1,0:T(8,128)} %get-tuple-element.211, bf16[128,256]{1,0:T(8,128)(2,1)S(1)} %get-tuple-element.210, bf16[2048,2048]{1,0:T(8,128)(2,1)} %get-tuple-element.209, s32[]{:T(128)S(6)} %select_n.23), kind=kOutput, calls=%fused_computation.4.clone.1 | convolution fusion | flops 137363456 | bytes 3735556 | tf_op jit(solution)/shard_map/while/body/eval_jaxpr/dot_general | solution.py:62
  162.9 2.5 %multiply_convert_fusion.3 = bf16[2048,256]{1,0:T(8,128)(2,1)S(1)} fusion(f32[2048,256]{1,0:T(8,128)} %get-tuple-element.211, bf16[128,256]{1,0:T(8,128)(2,1)S(1)} %get-tuple-element.210, bf16[2048,2048]{1,0:T(8,128)(2,1)} %get-tuple-element.209, s32[]{:T(128)S(6)} %select_n.23), kind=kOutput, calls=%fused_computation.4.clone.1 | convolution fusion | flops 137363456 | bytes 3735556 | tf_op jit(solution)/shard_map/while/body/eval_jaxpr/dot_general | solution.py:62
  172.5 2.5 %multiply_convert_fusion.3 = bf16[2048,256]{1,0:T(8,128)(2,1)S(1)} fusion(f32[2048,256]{1,0:T(8,128)} %get-tuple-element.211, bf16[128,256]{1,0:T(8,128)(2,1)S(1)} %get-tuple-element.210, bf16[2048,2048]{1,0:T(8,128)(2,1)} %get-tuple-element.209, s32[]{:T(128)S(6)} %select_n.23), kind=kOutput, calls=%fused_computation.4.clone.1 | convolution fusion | flops 137363456 | bytes 3735556 | tf_op jit(solution)/shard_map/while/body/eval_jaxpr/dot_general | solution.py:62
  177.7 28.6 %all-to-all-start.2 = ((f32[32,1,2048]{2,1,0:T(1,128)}), f32[32,1,2048]{2,1,0:T(1,128)S(1)}, u32[]{:S(2)}, u32[]{:S(2)}) async-start(f32[32,1,2048]{2,1,0:T(1,128)} %broadcast_in_dim.36), calls=%async_computation.2 | async-start | bytes 524288 | tf_op jit(solution)/shard_map/all_to_all | solution.py:13
  206.6 10.9 %all-to-all-done.2 = f32[32,1,2048]{2,1,0:T(1,128)S(1)} async-done(((f32[32,1,2048]{2,1,0:T(1,128)}), f32[32,1,2048]{2,1,0:T(1,128)S(1)}, u32[]{:S(2)}, u32[]{:S(2)}) %all-to-all-start.2) | async-done | bytes 262176 | tf_op jit(solution)/shard_map/all_to_all | solution.py:13
  218.9 12.4 %all_to_all.34 = f32[8,1,17]{2,1,0:T(1,128)S(1)} all-to-all(f32[8,1,17]{2,1,0:T(1,128)S(1)} %broadcast_in_dim.37), channel_id=1, replica_groups=mesh['mkt'=8,'trade'=8,'scen'=4] {'trade'}, dimensions={0} | all-to-all | bytes 1088 | tf_op jit(solution)/shard_map/all_to_all | solution.py:13
  (155 shorter events, 70.3 us)
Async XLA Ops:
  0.6 33.4 %copy-start = (bf16[16,128,128]{2,1,0:T(8,128)(2,1)S(1)}, bf16[16,128,128]{2,1,0:T(8,128)(2,1)}, u32[]{:S(2)}) copy-start(bf16[16,128,128]{2,1,0:T(8,128)(2,1)} %param.13) | copy-start | bytes 1572868
  49.2 39.4 %all-to-all-start.1 = ((bf16[8,64,2048]{2,1,0:T(8,128)(2,1)}), bf16[8,64,2048]{2,1,0:T(8,128)(2,1)S(1)}, u32[]{:S(2)}, u32[]{:S(2)}) async-start(bf16[8,64,2048]{2,1,0:T(8,128)(2,1)} %broadcast_in_dim.34), calls=%async_computation.1 | async-start | bytes 4194304 | tf_op jit(solution)/shard_map/all_to_all | solution.py:13
  57.3 3.4 %copy-start.3 = (s32[2048]{0:T(1024)S(1)}, s32[2048]{0:T(1024)}, u32[]{:S(2)}) copy-start(s32[2048]{0:T(1024)} %param.14) | copy-start | bytes 24580
  88.6 11.0 %copy-start.6 = (bf16[256,256]{1,0:T(8,128)(2,1)S(1)}, bf16[256,256]{1,0:T(8,128)(2,1)}, u32[]{:S(2)}) copy-start(bf16[256,256]{1,0:T(8,128)(2,1)} %param.19) | copy-start | bytes 393220
  88.6 11.0 %copy-start.7 = (bf16[128,256]{1,0:T(8,128)(2,1)S(1)}, bf16[128,256]{1,0:T(8,128)(2,1)}, u32[]{:S(2)}) copy-start(bf16[128,256]{1,0:T(8,128)(2,1)} %param.18) | copy-start | bytes 196612
  88.6 11.0 %copy-start.8 = (f32[256]{0:T(256)S(1)}, f32[256]{0:T(256)}, u32[]{:S(2)}) copy-start(f32[256]{0:T(256)} %param.20) | copy-start | bytes 3076
  88.6 11.0 %copy-start.9 = (bf16[256]{0:T(256)(128)(2,1)S(1)}, bf16[256]{0:T(256)(128)(2,1)}, u32[]{:S(2)}) copy-start(bf16[256]{0:T(256)(128)(2,1)} %param.21) | copy-start | bytes 1540
  99.6 76.4 %copy-start.4 = (s32[16]{0:T(128)S(1)}, s32[16]{0:T(128)}, u32[]{:S(2)}) copy-start(s32[16]{0:T(128)} %param.17) | copy-start | bytes 196
  99.6 106.7 %copy-start.1 = (f32[2048]{0:T(1024)S(1)}, f32[2048]{0:T(1024)}, u32[]{:S(2)}) copy-start(f32[2048]{0:T(1024)} %param.16) | copy-start | bytes 24580
  177.7 39.7 %all-to-all-start.2 = ((f32[32,1,2048]{2,1,0:T(1,128)}), f32[32,1,2048]{2,1,0:T(1,128)S(1)}, u32[]{:S(2)}, u32[]{:S(2)}) async-start(f32[32,1,2048]{2,1,0:T(1,128)} %broadcast_in_dim.36), calls=%async_computation.2 | async-start | bytes 524288 | tf_op jit(solution)/shard_map/all_to_all | solution.py:13
  217.6 14.4 %copy-start.2 = (f32[2048]{0:T(1024)}, f32[2048]{0:T(1024)S(1)}, u32[]{:S(2)}) copy-start(f32[2048]{0:T(1024)S(1)} %reduce_sum.28) | copy-start | bytes 24580
  231.4 0.6 copy-start.5
where the time goes:
time: 234 us; the launch traced here: 232 us
  local copies, waits for them, and re-layouts  59.7 us (26%)
  matrix products  54.5 us (23%)
  waiting for transfers between devices  38.8 us (17%)
  starting transfers between devices  36.7 us (16%)
  blocking collectives  25.5 us (11%)
  loops' own time  11.1 us (5%)
  other arithmetic  4.88 us (2%)
    dot_general x16, matrix products, price(): jnp.dot(trade_rows, w_in, preferred_element_type=jnp.float32) + embed_float  39.9 us
    all_to_all x2, waiting for transfers between devices, copy_for_each(): lax.all_to_all(jnp.broadcast_to(x[None], (size, *x.shape)), axis, 0, 0, t...  38.8 us
    all_to_all x2, starting transfers between devices, copy_for_each(): lax.all_to_all(jnp.broadcast_to(x[None], (size, *x.shape)), axis, 0, 0, t...  36.7 us
    gather x48, local copies, waits for them, and re-layouts  33.3 us
    dot_general x16, matrix products, price(): return jnp.dot(hidden_two, w_out, preferred_element_type=jnp.float32)  13.2 us
    all_to_all x1, blocking collectives, local(): lax.all_to_all(built_state, 'scen', split_axis=1, concat_axis=0, tiled=True)  13.1 us
    all_to_all x1, blocking collectives, copy_for_each(): lax.all_to_all(jnp.broadcast_to(x[None], (size, *x.shape)), axis, 0, 0, t...  12.4 us
    another operation x1, loops' own time, local(): values = lax.map(price, jnp.arange(scen_count, dtype=jnp.int32))  11.1 us
  transfers between devices with their start and end apart: 2, of which 2 were waited for; matrix products, arithmetic and copies ran while one was open for 2% of the time, Pallas kernels for 0%

commit v1 on v0

v1 whole, which is shorter than its diff:
```python
import functools
import math

import jax
import jax.numpy as jnp
from jax import lax
from jax.experimental import pallas as pl
from jax.experimental.pallas import tpu as pltpu
from jax.sharding import PartitionSpec as P

SEG = 128
WIN = 128
QSTEP = 8
HIGHEST = lax.Precision.HIGHEST
UNROLL = 4


def copy_for_each(x, axis):
    size = lax.axis_size(axis)
    return lax.all_to_all(jnp.broadcast_to(x[None], (size, *x.shape)), axis, 0, 0, tiled=True)


def of_everyone(x, axis):
    return copy_for_each(x, axis).sum(axis=0)


def prepare(w_in, w_mid, b_mid, w_out, embed, e32, w1, w2t, b2, w3):
    w1[...] = (w_in[...].astype(jnp.float32) * 0.5).astype(jnp.bfloat16)
    w2t[...] = (w_mid[...].astype(jnp.float32).T * 0.5).astype(jnp.bfloat16)
    b2[...] = jnp.broadcast_to(b_mid[...].reshape(1, -1) * 0.5, b2.shape[::-1]).T
    w3[...] = jnp.broadcast_to(w_out[...].reshape(1, -1), w3.shape)

    @pl.loop(0, embed.shape[0] // 64)
    def _(i):
        r = pl.multiple_of(i * 64, 64)
        t = embed[pl.ds(r, 64), :].astype(jnp.float32) * 0.5
        e32[0, pl.ds(r, 64), :] = t[:, :128]
        e32[1, pl.ds(r, 64), :] = t[:, 128:]


def price(idx, table, e32, w1, w2t, b2, w3, h1, h2, values):
    groups = values.shape[0]
    u_count = UNROLL

    def first(g, slot):
        x = jnp.concatenate([table[idx[j * groups + g]] for j in range(16)], axis=0)
        e = jnp.concatenate(
            [
                jnp.concatenate([e32.at[h][pl.ds(j * groups + g, 16, stride=0), :] for j in range(16)], axis=0)
                for h in range(2)
            ],
            axis=1,
        )
        z = jnp.dot(x, w1[...], preferred_element_type=jnp.float32) + e
        h1[slot] = (z + z * jnp.tanh(z)).astype(jnp.bfloat16)

    def second(slot):
        z = lax.dot_general(w2t[...], h1[slot], (((1,), (1,)), ((), ())), preferred_element_type=jnp.float32)
        z = z + b2[...]
        h2[slot] = (z + z * jnp.tanh(z)).astype(jnp.bfloat16)

    def third(g, slot):
        v = jnp.dot(w3[...], h2[slot], preferred_element_type=jnp.float32)
        values[pl.ds(g, 1), :] = v[0:1, :]

    def half(i, a, b):
        for u in range(u_count):
            first(jnp.minimum((i + 2) * u_count + u, groups - 1), a + u)
            second(b + u)
            third(i * u_count + u, a + u)

    for u in range(u_count):
        first(u, u)
    for u in range(u_count):
        second(u)
        first(u_count + u, u_count + u)

    @pl.loop(0, groups // u_count // 2)
    def _(k):
        half(2 * k, 0, u_count)
        half(2 * k + 1, u_count, 0)


def reduce_values(rank, position, values, span, weight_sum, marg, pnl):
    groups, width = values.shape
    row = lax.broadcasted_iota(jnp.int32, (16, width), 0)
    lane = lax.broadcasted_iota(jnp.int32, (16, width), 1)
    ranks = jnp.zeros((16, width), jnp.float32)
    for s in range(16):
        ranks = jnp.where(lane % 16 == s, rank[s].astype(jnp.float32), ranks)
    weights = jnp.exp(-ranks / span) * (1.0 / weight_sum)
    mine = row == lane // 16
    v = values[...]
    marg[...] = -lax.dot_general(
        jnp.where(mine, weights, 0.0), v, (((1,), (1,)), ((), ())),
        precision=HIGHEST, preferred_element_type=jnp.float32,
    )
    spread = jnp.dot(
        position[...].T, jnp.where(mine, 1.0, 0.0), precision=HIGHEST, preferred_element_type=jnp.float32
    )
    held = jnp.sum(v * spread, axis=0, keepdims=True)
    fold = (
        lax.broadcasted_iota(jnp.int32, (width, 128), 0) % 16 == lax.broadcasted_iota(jnp.int32, (width, 128), 1)
    )
    pnl[...] = jnp.dot(
        jnp.broadcast_to(held, (8, width)), jnp.where(fold, 1.0, 0.0),
        precision=HIGHEST, preferred_element_type=jnp.float32,
    )


def pricing_kernel(
    span, weight_sum, idx, rank, table, embed, position, w_in, w_mid, b_mid, w_out, marg, pnl,
    e32, w1, w2t, b2, w3, h1, h2, values,
):
    prepare(w_in, w_mid, b_mid, w_out, embed, e32, w1, w2t, b2, w3)
    price(idx, table, e32, w1, w2t, b2, w3, h1, h2, values)
    reduce_values(rank, position, values, span, weight_sum, marg, pnl)


def local(quotes, kernel, trade_block, trade_embed, position, scen_rank, w_in, w_mid, b_mid, w_out):
    local_count = kernel.shape[0]
    rows, quote_count = quotes.shape
    part = lax.axis_index(("trade", "scen"))
    block = part * local_count + jnp.arange(local_count, dtype=jnp.int32)
    start = jnp.clip(QSTEP * block - (WIN - QSTEP) // 2, 0, quote_count - WIN)
    base = jnp.clip((part - 1) * 128, 0, quote_count - 384)
    slab = lax.dynamic_slice_in_dim(quotes, base, 384, 1)
    pick = (
        jnp.arange(384, dtype=jnp.int32)[:, None]
        == ((start - base)[:, None] + jnp.arange(WIN, dtype=jnp.int32)[None, :]).reshape(1, -1)
    )
    windows = jnp.dot(slab, pick.astype(jnp.bfloat16), preferred_element_type=jnp.float32).astype(jnp.bfloat16)
    windows = windows.reshape(rows, local_count, WIN).transpose(1, 0, 2)
    built = jnp.einsum("jrw,jws->jrs", windows, kernel, preferred_element_type=jnp.float32)
    built = built.astype(jnp.bfloat16).reshape(local_count, rows * SEG)
    quarter = lax.all_to_all(built, "scen", split_axis=1, concat_axis=0, tiled=True)
    table = copy_for_each(quarter, "trade").reshape(-1, 16, SEG)

    scen_total = scen_rank.shape[0] * lax.axis_size("mkt") * lax.axis_size("scen")
    span = scen_total // 20
    weight_sum = math.fsum(math.exp(-r / span) for r in range(scen_total))
    trades, hid = trade_embed.shape
    groups = trades // 16
    slots = 2 * UNROLL
    vmem, smem = pl.BlockSpec(memory_space=pltpu.VMEM), pl.BlockSpec(memory_space=pltpu.SMEM)
    marg, pnl = pl.pallas_call(
        functools.partial(pricing_kernel, span, weight_sum),
        out_shape=(
            jax.ShapeDtypeStruct((16, groups), jnp.float32),
            jax.ShapeDtypeStruct((8, 128), jnp.float32),
        ),
        in_specs=[smem, smem] + [vmem] * 7,
        out_specs=(vmem, vmem),
        scratch_shapes=[
            pltpu.VMEM((2, trades, 128), jnp.float32),
            pltpu.VMEM((SEG, hid), jnp.bfloat16),
            pltpu.VMEM((hid, hid), jnp.bfloat16),
            pltpu.VMEM((hid, 256), jnp.float32),
            pltpu.VMEM((16, hid), jnp.bfloat16),
            pltpu.VMEM((slots, 256, hid), jnp.bfloat16),
            pltpu.VMEM((slots, hid, 256), jnp.bfloat16),
            pltpu.VMEM((groups, 256), jnp.float32),
        ],
        compiler_params=pltpu.CompilerParams(vmem_limit_bytes=48 << 20),
        name="price",
    )(trade_block, scen_rank, table, trade_embed, position.reshape(16, groups), w_in, w_mid, b_mid, w_out)

    marginal = of_everyone(marg, ("mkt", "scen"))
    own_share = jnp.sum(position * marginal.reshape(-1))
    both = of_everyone(jnp.concatenate([pnl[0, :16], own_share[None]]), "trade")
    return (both[:16], marginal.reshape(-1), both[16])


def solution(mesh):
    placed = (
        P("mkt", None),
        P(("trade", "scen"), None, None),
        P("trade"),
        P("trade", None),
        P("trade"),
        P(("mkt", "scen")),
        P(),
        P(),
        P(),
        P(),
    )
    return jax.shard_map(
        local,
        mesh=mesh,
        in_specs=placed,
        out_specs=(P(("mkt", "scen")), P("trade"), P()),
        check_vma=False,
    )
```

time: 234 us -> 129 us (0.55)
  local copies, waits for them, and re-layouts: 59.7 us -> 3.93 us
  matrix products: 54.5 us -> 2.05 us
  blocking collectives: 25.5 us -> 65 us
  waiting for transfers between devices: 38.8 us -> 11.1 us
  Pallas kernels: 0 us -> 16 us
  loops' own time: 11.1 us -> 0 us
  starting transfers between devices: 36.7 us -> 28.6 us
  other arithmetic: 4.88 us -> 1.46 us
    dot_general x34 -> x1, matrix products: 54.2 us -> 0.75 us  [local(): jnp.dot(slab, pick.astype(jnp.bfloat16), preferred_element_type=jnp.float32)]
    gather x49 -> x0, local copies, waits for them, and re-layouts: 44.2 us -> none
    all_to_all x1 -> x2, blocking collectives: 12.4 us -> 52 us  [copy_for_each(): lax.all_to_all(jnp.broadcast_to(x[None], (size, *x.shape)), axis, 0, 0, t...]
    all_to_all x2 -> x1, waiting for transfers between devices: 38.8 us -> 11.1 us  [copy_for_each(): lax.all_to_all(jnp.broadcast_to(x[None], (size, *x.shape)), axis, 0, 0, t...]
    pallas_call x0 -> x1, Pallas kernels: none -> 16 us  [local(): pl.pallas_call(functools.partial(pricing_kernel, span, weight_sum), out_s...]
    another operation x2 -> x0, loops' own time: 11.1 us -> none  [the longest x1 11.1 us: local(): values = lax.map(price, jnp.arange(scen_count, dtype=jnp.int32))]
    dynamic_slice x16 -> x0, local copies, waits for them, and re-layouts: 9.38 us -> none  [local(): values = lax.map(price, jnp.arange(scen_count, dtype=jnp.int32))]
    all_to_all x2 -> x1, starting transfers between devices: 36.7 us -> 28.6 us  [copy_for_each(): lax.all_to_all(jnp.broadcast_to(x[None], (size, *x.shape)), axis, 0, 0, t...]
  transfers between devices with their start and end apart: 2 -> 1, of which waited for: 2 -> 1; matrix products, arithmetic and copies ran while one was open for 2% -> 0% of each run, Pallas kernels for 0% -> 0%
where the time goes in v1:
time: 129 us
  blocking collectives  65 us (50%)
  starting transfers between devices  28.6 us (22%)
  Pallas kernels  16 us (12%)
  waiting for transfers between devices  11.1 us (9%)
  local copies, waits for them, and re-layouts  3.93 us (3%)
  matrix products  2.05 us (2%)
  other arithmetic  1.46 us (1%)
    all_to_all x2, blocking collectives, copy_for_each(): lax.all_to_all(jnp.broadcast_to(x[None], (size, *x.shape)), axis, 0, 0, t...  52 us
    all_to_all x1, starting transfers between devices, copy_for_each(): lax.all_to_all(jnp.broadcast_to(x[None], (size, *x.shape)), axis, 0, 0, t...  28.6 us
    pallas_call x1, Pallas kernels, local(): pl.pallas_call(functools.partial(pricing_kernel, span, weight_sum), out_s...  16 us
    all_to_all x1, blocking collectives, local(): lax.all_to_all(built, 'scen', split_axis=1, concat_axis=0, tiled=True)  13.1 us
    all_to_all x1, waiting for transfers between devices, copy_for_each(): lax.all_to_all(jnp.broadcast_to(x[None], (size, *x.shape)), axis, 0, 0, t...  11.1 us
  transfers between devices with their start and end apart: 1, of which 1 were waited for; matrix products, arithmetic and copies ran while one was open for 0% of the time, Pallas kernels for 0%

profile of v1, /device:TPU:1, one launch (start us, length us, event | category | flops | bytes accessed | tf_op | source)
XLA Modules:
  0.0 128.9 jit_solution(8328470209808155374)
XLA Ops:
  0.6 0.0 copy-start
  0.7 0.1 add_bitcast_fusion
  0.7 0.9 copy-done
  1.7 0.7 fusion.3
  2.4 1.3 %convolution_convert_fusion = bf16[16,64,128]{2,1,0:T(8,128)(2,1)S(1)} fusion(bf16[16,128,128]{2,1,0:T(8,128)(2,1)} %param.11, bf16[8,16,8,128]{3,2,1,0:T(8,128)(2,1)S(1)} %fusion.3), kind=kOutput, calls=%fused_computation.4 | convolution fusion | flops 33685504 | bytes 1048576 | tf_op jit(solution)/shard_map/jrw,jws->jrs/dot_general | solution.py:134
  3.7 0.1 all_to_all.22
  3.8 0.2 copy.19
  4.0 13.1 %all_to_all.32 = bf16[16,4,2048]{2,0,1:T(8,128)(2,1)S(1)} all-to-all(bf16[16,4,2048]{2,0,1:T(8,128)(2,1)S(1)} %copy.19), channel_id=1, replica_groups=mesh['mkt'=8,'trade'=8,'scen'=4] {'scen'}, dimensions={1} | all-to-all | bytes 524288 | tf_op jit(solution)/shard_map/all_to_all | solution.py:136
  17.0 0.2 broadcast_in_dim.11
  17.3 39.2 %all_to_all.33 = bf16[8,64,2048]{2,1,0:T(8,128)(2,1)S(1)} all-to-all(bf16[8,64,2048]{2,1,0:T(8,128)(2,1)S(1)} %broadcast_in_dim.11), channel_id=1, replica_groups=mesh['mkt'=8,'trade'=8,'scen'=4] {'trade'}, dimensions={0} | all-to-all | bytes 4194304 | tf_op jit(solution)/shard_map/all_to_all | solution.py:20
  56.5 0.0 copy-start.5
  56.5 0.0 copy-start.7
  56.6 0.0 copy-start.8
  56.6 0.6 copy.22
  57.2 0.6 copy-done.1
  57.8 16.0 %price.1 = (f32[16,128]{1,0:T(8,128)S(1)}, f32[8,128]{1,0:T(8,128)S(1)}) custom-call(s32[2048]{0:T(1024)S(1)} %copy-done.5, s32[16]{0:T(128)S(1)} %copy-done.7, bf16[512,16,128]{2,1,0:T(8,128)(2,1)S(1)} %bitcast.26, bf16[2048,256]{1,0:T(8,128)(2,1)S(1)} %copy-done.1, f32[16,128]{1,0:T(8,128)S(1)} %bitcast.27, bf16[128,256]{1,0:T(8,128)(2,1)S(1)} %copy-done.3, ...), custom_call_target="tpu_custom_call" | custom-call | tf_op jit(solution)/shard_map/price/pallas_call | solution.py:146
  73.8 0.7 broadcast_in_dim.12
  74.5 28.6 %all-to-all-start.2 = ((f32[32,16,128]{2,1,0:T(8,128)}), f32[32,16,128]{2,1,0:T(8,128)S(1)}, u32[]{:S(2)}, u32[]{:S(2)}) async-start(f32[32,16,128]{2,1,0:T(8,128)} %broadcast_in_dim.12), calls=%async_computation.2 | async-start | bytes 524288 | tf_op jit(solution)/shard_map/all_to_all | solution.py:20
  103.1 11.1 %all-to-all-done.2 = f32[32,16,128]{2,1,0:T(8,128)S(1)} async-done(((f32[32,16,128]{2,1,0:T(8,128)}), f32[32,16,128]{2,1,0:T(8,128)S(1)}, u32[]{:S(2)}, u32[]{:S(2)}) %all-to-all-start.2) | async-done | bytes 262176 | tf_op jit(solution)/shard_map/all_to_all | solution.py:20
  114.2 0.0 copy-start.9
  114.2 0.6 multiply_reduce_fusion
  114.8 0.7 pad_maximum_fusion
  115.6 12.7 %all_to_all.34 = f32[8,1,17]{2,1,0:T(1,128)S(1)} all-to-all(f32[8,1,17]{2,1,0:T(1,128)S(1)} %broadcast_in_dim.14), channel_id=1, replica_groups=mesh['mkt'=8,'trade'=8,'scen'=4] {'trade'}, dimensions={0} | all-to-all | bytes 1088 | tf_op jit(solution)/shard_map/all_to_all | solution.py:20
  128.3 0.6 slice.11
  (20 shorter events, 0.1 us)
Async XLA Ops:
  0.6 1.0 copy-start
  56.5 1.2 copy-start.1
  56.5 1.2 copy-start.2
  56.5 1.2 copy-start.3
  56.5 1.2 copy-start.4
  56.5 1.2 copy-start.5
  56.5 1.2 copy-start.6
  56.5 1.2 copy-start.7
  56.6 1.2 copy-start.8
  74.5 39.7 %all-to-all-start.2 = ((f32[32,16,128]{2,1,0:T(8,128)}), f32[32,16,128]{2,1,0:T(8,128)S(1)}, u32[]{:S(2)}, u32[]{:S(2)}) async-start(f32[32,16,128]{2,1,0:T(8,128)} %broadcast_in_dim.12), calls=%async_computation.2 | async-start | bytes 524288 | tf_op jit(solution)/shard_map/all_to_all | solution.py:20
  114.2 14.7 %copy-start.9 = (f32[16,128]{1,0:T(8,128)}, f32[16,128]{1,0:T(8,128)S(1)}, u32[]{:S(2)}) copy-start(f32[16,128]{1,0:T(8,128)S(1)} %reduce_sum.27) | copy-start | bytes 24580
  128.3 0.6 copy-start.10

commit v2 on v1

--- a/solution.py
+++ b/solution.py
@@ -11,17 +11,10 @@
 SEG = 128
 WIN = 128
 QSTEP = 8
+SLAB = 384
 HIGHEST = lax.Precision.HIGHEST
+MESH = pl.DeviceIdType.MESH
 UNROLL = 4
-
-
-def copy_for_each(x, axis):
-    size = lax.axis_size(axis)
-    return lax.all_to_all(jnp.broadcast_to(x[None], (size, *x.shape)), axis, 0, 0, tiled=True)
-
-
-def of_everyone(x, axis):
-    return copy_for_each(x, axis).sum(axis=0)
 
 
 def prepare(w_in, w_mid, b_mid, w_out, embed, e32, w1, w2t, b2, w3):
@@ -91,7 +84,7 @@
     weights = jnp.exp(-ranks / span) * (1.0 / weight_sum)
     mine = row == lane // 16
     v = values[...]
-    marg[...] = -lax.dot_general(
+    marg[0:16] = -lax.dot_general(
         jnp.where(mine, weights, 0.0), v, (((1,), (1,)), ((), ())),
         precision=HIGHEST, preferred_element_type=jnp.float32,
     )
@@ -99,6 +92,7 @@
         position[...].T, jnp.where(mine, 1.0, 0.0), precision=HIGHEST, preferred_element_type=jnp.float32
     )
     held = jnp.sum(v * spread, axis=0, keepdims=True)
+    marg[16:24] = jnp.broadcast_to(-jnp.sum(held * weights[0:1], axis=1, keepdims=True), (8, groups))
     fold = (
         lax.broadcasted_iota(jnp.int32, (width, 128), 0) % 16 == lax.broadcasted_iota(jnp.int32, (width, 128), 1)
     )
@@ -108,34 +102,160 @@
     )
 
 
-def pricing_kernel(
-    span, weight_sum, idx, rank, table, embed, position, w_in, w_mid, b_mid, w_out, marg, pnl,
-    e32, w1, w2t, b2, w3, h1, h2, values,
+def build(slab, kernel, offset, built, table, part, scen):
+    rows = slab.shape[0]
+    for j in range(kernel.shape[0]):
+        pick = lax.broadcasted_iota(jnp.int32, (SLAB, WIN), 0) == lax.broadcasted_iota(jnp.int32, (SLAB, WIN), 1) + offset(j)
+        window = jnp.dot(
+            slab[...], jnp.where(pick, 1.0, 0.0).astype(jnp.bfloat16), preferred_element_type=jnp.float32
+        ).astype(jnp.bfloat16)
+        state = jnp.dot(window, kernel[j], preferred_element_type=jnp.float32).astype(jnp.bfloat16)
+        for q in range(rows // 16):
+            built[q, j] = state[16 * q : 16 * q + 16]
+
+
+def fused_kernel(
+    span, weight_sum, quote_count,
+    quotes_hbm, kernel_hbm, embed_hbm, idx, rank, position, w_in, w_mid, b_mid, w_out,
+    marg_out, pnl_out, short_out,
+    slab, kernel, embed, built, table, e32, w1, w2t, b2, w3, h1, h2, values, msg, pnl,
+    got_mkt, got_pnl, got_marg, got_short, load_sem, z_send, y_send, recv, t_send, r_mkt, r_pnl, r_marg, r_short,
 ):
-    prepare(w_in, w_mid, b_mid, w_out, embed, e32, w1, w2t, b2, w3)
+    mkt, trade, scen = lax.axis_index("mkt"), lax.axis_index("trade"), lax.axis_index("scen")
+    y, z_hi = trade // 2, trade % 2
+    z = z_hi * 4 + scen
+    part = y * 8 + z
+    blocks = kernel.shape[0]
+
+    def at_z(zz):
+        return {"trade": y * 2 + zz // 4, "scen": zz % 4}
+
+    def at_y(yy):
+        return {"trade": yy * 2 + z_hi}
+
+    base = jnp.clip((part - 1) * 128, 0, quote_count - SLAB)
+    loads = [
+        pltpu.make_async_copy(quotes_hbm.at[:, pl.ds(pl.multiple_of(base, 128), SLAB)], slab, load_sem.at[0]),
+        pltpu.make_async_copy(kernel_hbm, kernel, load_sem.at[1]),
+        pltpu.make_async_copy(embed_hbm, embed, load_sem.at[2]),
+    ]
+    for load in loads:
+        load.start()
+
+    barrier = pltpu.get_barrier_semaphore()
+    for k in range(1, 8):
+        pl.semaphore_signal(barrier, inc=1, device_id={"mkt": (mkt + k) % 8}, device_id_type=MESH)
+    for k in range(1, 32):
+        other = (part + k) % 32
+        pl.semaphore_signal(
+            barrier, inc=1, device_id={"trade": other // 4, "scen": other % 4}, device_id_type=MESH
+        )
+
+    def offset(j):
+        return jnp.clip(QSTEP * (part * blocks + j) - (WIN - QSTEP) // 2, 0, quote_count - WIN) - base
+
+    loads[0].wait()
+    loads[1].wait()
+    build(slab, kernel, offset, built, table, part, scen)
+    table[pl.ds(part * blocks, blocks)] = built[scen]
+    pl.semaphore_wait(barrier, 38)
+
+    def piece(p):
+        return table.at[pl.ds(p * blocks, blocks)]
+
+    def copy(src, dst, send, receive, device):
+        return pltpu.make_async_remote_copy(
+            src_ref=src, dst_ref=dst, send_sem=send, recv_sem=receive, device_id=device, device_id_type=MESH
+        )
+
+    sends = []
+
+    def send(*args):
+        c = copy(*args)
+        c.start()
+        sends.append(c)
+
+    def await_piece(p):
+        copy(piece(p), piece(p), y_send.at[0], recv.at[p], at_y((y + 1) % 4)).wait_recv()
+
+    steps = (1, 7, 2, 6, 3, 5, 4)
+    for k, d in enumerate(steps):
+        to = (z + d) % 8
+        send(built.at[to % 4], piece(part), z_send.at[k], recv.at[part], at_z(to))
+    up, down = (y + 1) % 4, (y + 3) % 4
+    arrivals = (0,) + tuple(8 - d for d in steps)
+    for k, d in enumerate(arrivals):
+        source = (z + d) % 8
+        p = y * 8 + source
+        if d:
+            await_piece(p)
+        send(piece(p), piece(p), y_send.at[3 * k], recv.at[p], at_y(up))
+        send(piece(p), piece(p), y_send.at[3 * k + 1], recv.at[p], at_y(down))
+        if k == 0:
+            loads[2].wait()
+            prepare(w_in, w_mid, b_mid, w_out, embed, e32, w1, w2t, b2, w3)
+        even = source % 2 == 0
+        near, far = jnp.where(even, down, up), jnp.where(even, up, down)
+        p = near * 8 + source
+        await_piece(p)
+        send(piece(p), piece(p), y_send.at[3 * k + 2], recv.at[p], at_y(far))
+    for d in arrivals:
+        source = (z + d) % 8
+        await_piece(jnp.where(source % 2 == 0, up, down) * 8 + source)
+        await_piece((y + 2) % 4 * 8 + source)
+
     price(idx, table, e32, w1, w2t, b2, w3, h1, h2, values)
-    reduce_values(rank, position, values, span, weight_sum, marg, pnl)
+    reduce_values(rank, position, values, span, weight_sum, msg, pnl)
+
+    got_mkt[mkt] = msg[...]
+    got_pnl[trade] = pnl[...]
+    for k in range(1, 8):
+        send(msg, got_mkt.at[mkt], t_send.at[k - 1], r_mkt.at[mkt], {"mkt": (mkt + k) % 8})
+    for k in range(1, 8):
+        send(pnl, got_pnl.at[trade], t_send.at[6 + k], r_pnl.at[trade], {"trade": (trade + k) % 8})
+    for k in range(1, 8):
+        other = (mkt + k) % 8
+        copy(msg, got_mkt.at[other], t_send.at[0], r_mkt.at[other], {"mkt": other}).wait_recv()
+    total = got_mkt[0]
+    for k in range(1, 8):
+        total = total + got_mkt[k]
+    got_marg[scen] = total[:16]
+    got_short[part] = total[16:]
+    for k in range(1, 32):
+        other = (part + k) % 32
+        send(
+            got_short.at[part], got_short.at[part], t_send.at[16 + k], r_short.at[part],
+            {"trade": other // 4, "scen": other % 4},
+        )
+    for k in range(1, 4):
+        send(got_marg.at[scen], got_marg.at[scen], t_send.at[13 + k], r_marg.at[scen], {"scen": (scen + k) % 4})
+    for k in range(1, 8):
+        other = (trade + k) % 8
+        copy(pnl, got_pnl.at[other], t_send.at[0], r_pnl.at[other], {"trade": other}).wait_recv()
+    total = got_pnl[0]
+    for k in range(1, 8):
+        total = total + got_pnl[k]
+    pnl_out[...] = total
+    for k in range(1, 4):
+        other = (scen + k) % 4
+        copy(got_marg.at[other], got_marg.at[other], t_send.at[0], r_marg.at[other], {"scen": other}).wait_recv()
+    marg_out[...] = (got_marg[0] + got_marg[1]) + (got_marg[2] + got_marg[3])
+    for k in range(1, 32):
+        other = (part + k) % 32
+        copy(
+            got_short.at[other], got_short.at[other], t_send.at[0], r_short.at[other], {"scen": scen}
+        ).wait_recv()
+    total = got_short[0]
+    for k in range(1, 32):
+        total = total + got_short[k]
+    short_out[...] = total
+    for c in sends:
+        c.wait_send()
 
 
 def local(quotes, kernel, trade_block, trade_embed, position, scen_rank, w_in, w_mid, b_mid, w_out):
-    local_count = kernel.shape[0]
     rows, quote_count = quotes.shape
-    part = lax.axis_index(("trade", "scen"))
-    block = part * local_count + jnp.arange(local_count, dtype=jnp.int32)
-    start = jnp.clip(QSTEP * block - (WIN - QSTEP) // 2, 0, quote_count - WIN)
-    base = jnp.clip((part - 1) * 128, 0, quote_count - 384)
-    slab = lax.dynamic_slice_in_dim(quotes, base, 384, 1)
-    pick = (
-        jnp.arange(384, dtype=jnp.int32)[:, None]
-        == ((start - base)[:, None] + jnp.arange(WIN, dtype=jnp.int32)[None, :]).reshape(1, -1)
-    )
-    windows = jnp.dot(slab, pick.astype(jnp.bfloat16), preferred_element_type=jnp.float32).astype(jnp.bfloat16)
-    windows = windows.reshape(rows, local_count, WIN).transpose(1, 0, 2)
-    built = jnp.einsum("jrw,jws->jrs", windows, kernel, preferred_element_type=jnp.float32)
-    built = built.astype(jnp.bfloat16).reshape(local_count, rows * SEG)
-    quarter = lax.all_to_all(built, "scen", split_axis=1, concat_axis=0, tiled=True)
-    table = copy_for_each(quarter, "trade").reshape(-1, 16, SEG)
-
+    blocks = kernel.shape[0]
     scen_total = scen_rank.shape[0] * lax.axis_size("mkt") * lax.axis_size("scen")
     span = scen_total // 20
     weight_sum = math.fsum(math.exp(-r / span) for r in range(scen_total))
@@ -143,32 +263,48 @@
     groups = trades // 16
     slots = 2 * UNROLL
     vmem, smem = pl.BlockSpec(memory_space=pltpu.VMEM), pl.BlockSpec(memory_space=pltpu.SMEM)
-    marg, pnl = pl.pallas_call(
-        functools.partial(pricing_kernel, span, weight_sum),
+    hbm = pl.BlockSpec(memory_space=pl.ANY)
+    bf16, f32 = jnp.bfloat16, jnp.float32
+    dma = pltpu.SemaphoreType.DMA
+    marg, pnl, short = pl.pallas_call(
+        functools.partial(fused_kernel, span, weight_sum, quote_count),
         out_shape=(
-            jax.ShapeDtypeStruct((16, groups), jnp.float32),
-            jax.ShapeDtypeStruct((8, 128), jnp.float32),
+            jax.ShapeDtypeStruct((16, groups), f32),
+            jax.ShapeDtypeStruct((8, 128), f32),
+            jax.ShapeDtypeStruct((8, 128), f32),
         ),
-        in_specs=[smem, smem] + [vmem] * 7,
-        out_specs=(vmem, vmem),
+        in_specs=[hbm, hbm, hbm, smem, smem] + [vmem] * 5,
+        out_specs=(vmem, vmem, vmem),
         scratch_shapes=[
-            pltpu.VMEM((2, trades, 128), jnp.float32),
-            pltpu.VMEM((SEG, hid), jnp.bfloat16),
-            pltpu.VMEM((hid, hid), jnp.bfloat16),
-            pltpu.VMEM((hid, 256), jnp.float32),
-            pltpu.VMEM((16, hid), jnp.bfloat16),
-            pltpu.VMEM((slots, 256, hid), jnp.bfloat16),
-            pltpu.VMEM((slots, hid, 256), jnp.bfloat16),
-            pltpu.VMEM((groups, 256), jnp.float32),
+            pltpu.VMEM((rows, SLAB), bf16),
+            pltpu.VMEM(kernel.shape, bf16),
+            pltpu.VMEM(trade_embed.shape, bf16),
+            pltpu.VMEM((rows // 16, blocks, 16, SEG), bf16),
+            pltpu.VMEM((32 * blocks, 16, SEG), bf16),
+            pltpu.VMEM((2, trades, 128), f32),
+            pltpu.VMEM((SEG, hid), bf16),
+            pltpu.VMEM((hid, hid), bf16),
+            pltpu.VMEM((hid, 256), f32),
+            pltpu.VMEM((16, hid), bf16),
+            pltpu.VMEM((slots, 256, hid), bf16),
+            pltpu.VMEM((slots, hid, 256), bf16),
+            pltpu.VMEM((groups, 256), f32),
+            pltpu.VMEM((24, groups), f32),
+            pltpu.VMEM((8, 128), f32),
+            pltpu.VMEM((8, 24, groups), f32),
+            pltpu.VMEM((8, 8, 128), f32),
+            pltpu.VMEM((4, 16, groups), f32),
+            pltpu.VMEM((32, 8, 128), f32),
+            dma((3,)), dma((7,)), dma((24,)), dma((32,)), dma((48,)), dma((8,)), dma((8,)), dma((4,)), dma((32,)),
         ],
-        compiler_params=pltpu.CompilerParams(vmem_limit_bytes=48 << 20),
-        name="price",
-    )(trade_block, scen_rank, table, trade_embed, position.reshape(16, groups), w_in, w_mid, b_mid, w_out)
-
-    marginal = of_everyone(marg, ("mkt", "scen"))
-    own_share = jnp.sum(position * marginal.reshape(-1))
-    both = of_everyone(jnp.concatenate([pnl[0, :16], own_share[None]]), "trade")
-    return (both[:16], marginal.reshape(-1), both[16])
+        compiler_params=pltpu.CompilerParams(
+            vmem_limit_bytes=48 << 20, collective_id=0, has_side_effects=True
+        ),
+        name="shortfall",
+    )(
+        quotes, kernel, trade_embed, trade_block, scen_rank, position.reshape(16, groups), w_in, w_mid, b_mid, w_out
+    )
+    return (pnl[0, :16], marg.reshape(-1), short[0, 0])
 
 
 def solution(mesh):

time: 129 us -> 87.2 us (0.68)
  blocking collectives: 65 us -> 0 us
  Pallas kernels: 16 us -> 76.7 us
  starting transfers between devices: 28.6 us -> 0 us
  waiting for transfers between devices: 11.1 us -> 0 us
  local copies, waits for them, and re-layouts: 3.93 us -> 9.39 us
  matrix products: 2.05 us -> 0 us
  other arithmetic: 1.46 us -> 0 us
    all_to_all x3 -> x0, blocking collectives: 65 us -> none  [the longest x2 52 us: copy_for_each(): lax.all_to_all(jnp.broadcast_to(x[None], (size, *x.shape)), axis, 0, 0, t...]
    pallas_call x1, Pallas kernels: 16 us -> 76.7 us  [local(): pl.pallas_call(functools.partial(fused_kernel, span, weight_sum, quote_co...]
    all_to_all x1 -> x0, starting transfers between devices: 28.6 us -> none  [copy_for_each(): lax.all_to_all(jnp.broadcast_to(x[None], (size, *x.shape)), axis, 0, 0, t...]
    all_to_all x1 -> x0, waiting for transfers between devices: 11.1 us -> none  [copy_for_each(): lax.all_to_all(jnp.broadcast_to(x[None], (size, *x.shape)), axis, 0, 0, t...]
    unnamed x23 -> x21, local copies, waits for them, and re-layouts: 2.15 us -> 8.36 us
    dot_general x2 -> x0, matrix products: 2.05 us -> none  [the longest x1 1.31 us: local(): jnp.einsum('jrw,jws->jrs', windows, kernel, preferred_element_type=jnp.fl...]
  transfers between devices with their start and end apart: 1 -> 0, of which waited for: 1 -> 0; matrix products, arithmetic and copies ran while one was open for 0% -> 0% of each run, Pallas kernels for 0% -> 0%
where the time goes in v2:
time: 87.2 us; the launch traced here: 86.8 us
  Pallas kernels  76.7 us (88%)
  local copies, waits for them, and re-layouts  9.39 us (11%)
    pallas_call x1, Pallas kernels, local(): pl.pallas_call(functools.partial(fused_kernel, span, weight_sum, quote_co...  76.7 us
    unnamed x21, local copies, waits for them, and re-layouts  8.36 us

profile of v2, /device:TPU:1, one launch (start us, length us, event | category | flops | bytes accessed | tf_op | source)
XLA Modules:
  0.0 86.8 jit_solution(12177041954503056766)
XLA Ops:
  0.6 0.0 copy-start.7
  0.6 0.0 copy-start.8
  0.7 0.7 copy-done.7
  1.3 0.0 copy-done.8
  1.3 0.0 copy-start
  1.3 1.2 %copy-done = bf16[2048,256]{1,0:T(8,128)(2,1)S(1)} copy-done((bf16[2048,256]{1,0:T(8,128)(2,1)S(1)}, bf16[2048,256]{1,0:T(8,128)(2,1)}, u32[]{:S(2)}) %copy-start) | copy-done | bytes 1048600
  2.5 0.0 copy-start.1
  2.5 1.0 %copy-done.1 = bf16[64,4096]{1,0:T(8,128)(2,1)S(1)} copy-done((bf16[64,4096]{1,0:T(8,128)(2,1)S(1)}, bf16[64,4096]{1,0:T(8,128)(2,1)}, u32[]{:S(2)}) %copy-start.1) | copy-done | bytes 524312
  3.6 0.0 copy-start.2
  3.6 1.0 %copy-done.2 = bf16[16,128,128]{2,1,0:T(8,128)(2,1)S(1)} copy-done((bf16[16,128,128]{2,1,0:T(8,128)(2,1)S(1)}, bf16[16,128,128]{2,1,0:T(8,128)(2,1)}, u32[]{:S(2)}) %copy-start.2) | copy-done | bytes 524312
  4.6 0.0 copy-start.3
  4.6 0.9 %copy-done.3 = bf16[256,256]{1,0:T(8,128)(2,1)S(1)} copy-done((bf16[256,256]{1,0:T(8,128)(2,1)S(1)}, bf16[256,256]{1,0:T(8,128)(2,1)}, u32[]{:S(2)}) %copy-start.3) | copy-done | bytes 131096
  5.5 0.0 copy-start.4
  5.5 0.8 copy-done.4
  6.4 0.0 copy-start.5
  6.4 0.7 copy-done.5
  7.1 0.0 copy-start.6
  7.1 0.7 copy-done.6
  7.8 0.0 copy-start.9
  7.8 0.7 copy-done.9
  8.4 76.7 %shortfall.1 = (f32[16,128]{1,0:T(8,128)S(1)}, f32[8,128]{1,0:T(8,128)S(1)}, f32[8,128]{1,0:T(8,128)S(1)}) custom-call(bf16[64,4096]{1,0:T(8,128)(2,1)S(1)} %copy-done.1, bf16[16,128,128]{2,1,0:T(8,128)(2,1)S(1)} %copy-done.2, bf16[2048,256]{1,0:T(8,128)(2,1)S(1)} %copy-done, s32[2048]{0:T(1024)S(1)} %copy-done.5, s32[16]{0:T(128)S(1)} %copy-done.8, ...), custom_call_target="tpu_custom_call" | custom-call | tf_op jit(solution)/shard_map/shortfall/pallas_call | solution.py:269
  85.2 0.5 slice.7
  85.7 0.5 slice_bitcast_fusion
  86.2 0.6 copy.14
Async XLA Ops:
  0.6 0.7 copy-start.7
  0.6 0.7 copy-start.8
  1.3 1.2 %copy-start = (bf16[2048,256]{1,0:T(8,128)(2,1)S(1)}, bf16[2048,256]{1,0:T(8,128)(2,1)}, u32[]{:S(2)}) copy-start(bf16[2048,256]{1,0:T(8,128)(2,1)} %embed_hbm.1) | copy-start | bytes 3145732
  2.5 1.0 %copy-start.1 = (bf16[64,4096]{1,0:T(8,128)(2,1)S(1)}, bf16[64,4096]{1,0:T(8,128)(2,1)}, u32[]{:S(2)}) copy-start(bf16[64,4096]{1,0:T(8,128)(2,1)} %quotes_hbm.1) | copy-start | bytes 1572868
  3.6 1.0 %copy-start.2 = (bf16[16,128,128]{2,1,0:T(8,128)(2,1)S(1)}, bf16[16,128,128]{2,1,0:T(8,128)(2,1)}, u32[]{:S(2)}) copy-start(bf16[16,128,128]{2,1,0:T(8,128)(2,1)} %kernel_hbm.1) | copy-start | bytes 1572868
  4.6 0.9 %copy-start.3 = (bf16[256,256]{1,0:T(8,128)(2,1)S(1)}, bf16[256,256]{1,0:T(8,128)(2,1)}, u32[]{:S(2)}) copy-start(bf16[256,256]{1,0:T(8,128)(2,1)} %w_mid.1) | copy-start | bytes 393220
  5.5 0.8 copy-start.4
  6.4 0.7 copy-start.5
  7.1 0.7 copy-start.6
  7.8 0.7 copy-start.9

commit v3 on v2

v3 whole, which is shorter than its diff:
```python
import functools
import math

import jax
import jax.numpy as jnp
from jax import lax
from jax.experimental import pallas as pl
from jax.experimental.pallas import tpu as pltpu
from jax.sharding import PartitionSpec as P

SEG = 128
WIN = 128
QSTEP = 8
SLAB = 384
LAG = 3
ORDER = (1, 7, 2, 6, 4, 3, 5)
HIGHEST = lax.Precision.HIGHEST
MESH = pl.DeviceIdType.MESH
UNROLL = 4


def prepare(w_in, w_mid, b_mid, w_out, embed, e32, w1, w2t, b2, w3):
    w1[...] = (w_in[...].astype(jnp.float32) * 0.5).astype(jnp.bfloat16)
    w2t[...] = (w_mid[...].astype(jnp.float32).T * 0.5).astype(jnp.bfloat16)
    b2[...] = jnp.broadcast_to(b_mid[...].reshape(1, -1) * 0.5, b2.shape[::-1]).T
    w3[...] = jnp.broadcast_to(w_out[...].reshape(1, -1), w3.shape)

    @pl.loop(0, embed.shape[0] // 64)
    def _(i):
        r = pl.multiple_of(i * 64, 64)
        t = embed[pl.ds(r, 64), :].astype(jnp.float32) * 0.5
        e32[0, pl.ds(r, 64), :] = t[:, :128]
        e32[1, pl.ds(r, 64), :] = t[:, 128:]


def price(half, idx, table, e32, w1, w2t, b2, w3, h1, h2, values, beside=lambda k: None):
    groups = values.shape[1] // 2
    u_count = UNROLL
    trades = [(c, j) for c in range(2) for j in range(16)]

    def row(g, c, j):
        return j * 2 * groups + c * groups + g

    def first(g, slot):
        x = jnp.concatenate([table[idx[row(g, c, j)]] for c, j in trades], axis=0).astype(jnp.bfloat16)
        e = jnp.concatenate(
            [
                jnp.concatenate([e32.at[i][pl.ds(row(g, c, j), 8, stride=0), :] for c, j in trades], axis=0)
                for i in range(2)
            ],
            axis=1,
        )
        z = jnp.dot(x, w1[...], preferred_element_type=jnp.float32) + e
        h1[slot] = (z + z * jnp.tanh(z)).astype(jnp.bfloat16)

    def second(slot):
        z = lax.dot_general(w2t[...], h1[slot], (((1,), (1,)), ((), ())), preferred_element_type=jnp.float32)
        z = z + b2[...]
        h2[slot] = (z + z * jnp.tanh(z)).astype(jnp.bfloat16)

    def third(g, slot):
        v = jnp.dot(w3[...], h2[slot], preferred_element_type=jnp.float32)
        values[half, pl.ds(g, 1), :] = v[0:1, :128]
        values[half, pl.ds(g + groups, 1), :] = v[0:1, 128:]

    def step(i, a, b):
        for u in range(u_count):
            first(jnp.minimum((i + 2) * u_count + u, groups - 1), a + u)
            second(b + u)
            third(i * u_count + u, a + u)

    for u in range(u_count):
        first(u, u)
    for u in range(u_count):
        second(u)
        first(u_count + u, u_count + u)

    @pl.loop(0, groups // u_count // 2)
    def _(k):
        beside(k)
        step(2 * k, 0, u_count)
        step(2 * k + 1, u_count, 0)


def prepare_reduce(rank, position, span, weight_sum, picked, spread):
    width = picked.shape[1]
    row = lax.broadcasted_iota(jnp.int32, (16, width), 0)
    lane = lax.broadcasted_iota(jnp.int32, (16, width), 1)
    ranks = jnp.zeros((16, width), jnp.float32)
    for s in range(16):
        ranks = jnp.where(lane // 128 * 8 + lane % 8 == s, rank[s].astype(jnp.float32), ranks)
    weights = jnp.exp(-ranks / span) * (1.0 / weight_sum)
    mine = row == lane % 128 // 8
    picked[0:16] = jnp.where(mine, weights, 0.0)
    picked[16:24] = weights[0:8]
    spread[...] = jnp.dot(
        position[...].T, jnp.where(mine, 1.0, 0.0), precision=HIGHEST, preferred_element_type=jnp.float32
    )


def reduce_values(values, picked, spread, marg, pnl):
    width = picked.shape[1]
    groups = values.shape[1]
    v = jnp.concatenate([values[0], values[1]], axis=1)
    marg[0:16] = -lax.dot_general(
        picked[0:16], v, (((1,), (1,)), ((), ())), precision=HIGHEST, preferred_element_type=jnp.float32
    )
    held = jnp.sum(v * spread[...], axis=0, keepdims=True)
    marg[16:24] = jnp.broadcast_to(-jnp.sum(held * picked[16:17], axis=1, keepdims=True), (8, groups))
    lane = lax.broadcasted_iota(jnp.int32, (width, 128), 0)
    fold = lane // 128 * 8 + lane % 8 == lax.broadcasted_iota(jnp.int32, (width, 128), 1)
    pnl[...] = jnp.dot(
        jnp.broadcast_to(held, (8, width)), jnp.where(fold, 1.0, 0.0),
        precision=HIGHEST, preferred_element_type=jnp.float32,
    )[0:1]


def build(slab, kernel, offset, built):
    for j in range(kernel.shape[0]):
        pick = lax.broadcasted_iota(jnp.int32, (SLAB, WIN), 0) == lax.broadcasted_iota(jnp.int32, (SLAB, WIN), 1) + offset(j)
        window = jnp.dot(
            slab[...], jnp.where(pick, 1.0, 0.0).astype(jnp.bfloat16), preferred_element_type=jnp.float32
        ).astype(jnp.bfloat16)
        state = jnp.dot(window, kernel[j], preferred_element_type=jnp.float32)
        for r in range(slab.shape[0] // 8):
            built[r % 2, r // 2, j] = state[8 * r : 8 * r + 8].astype(jnp.bfloat16)


def fused_kernel(
    span, weight_sum, quote_count,
    quotes_hbm, kernel_hbm, embed_hbm, idx_hbm, rank_hbm, position_hbm, w_in_hbm, w_mid_hbm, b_mid_hbm, w_out_hbm,
    marg_out, pnl_out, short_out,
    slab, kernel, embed, idx, rank, position, w_in, w_mid, b_mid, w_out, spread, picked, built, landed, table, e32, w1, w2t, b2, w3, h1, h2, values, msg, pnl,
    got_mkt, got_pnl, got_marg, got_short, load_sem, z_send, y_send, recv, t_send, r_mkt, r_pnl, r_marg, r_short,
):
    mkt, trade, scen = lax.axis_index("mkt"), lax.axis_index("trade"), lax.axis_index("scen")
    y, z_hi = trade // 2, trade % 2
    z = z_hi * 4 + scen
    part = y * 8 + z
    blocks = kernel.shape[0]

    def at_z(zz):
        return {"trade": y * 2 + zz // 4, "scen": zz % 4}

    def at_y(yy):
        return {"trade": yy * 2 + z_hi}

    base = jnp.clip((part - 1) * 128, 0, quote_count - SLAB)
    loads = [
        pltpu.make_async_copy(quotes_hbm.at[:, pl.ds(pl.multiple_of(base, 128), SLAB)], slab, load_sem.at[0]),
        pltpu.make_async_copy(kernel_hbm, kernel, load_sem.at[1]),
    ] + [
        pltpu.make_async_copy(src, dst, load_sem.at[2 + i])
        for i, (src, dst) in enumerate(
            [
                (embed_hbm, embed), (idx_hbm, idx), (rank_hbm, rank), (position_hbm, position),
                (w_in_hbm, w_in), (w_mid_hbm, w_mid), (b_mid_hbm, b_mid), (w_out_hbm, w_out),
            ]
        )
    ]
    for load in loads:
        load.start()

    barrier = pltpu.get_barrier_semaphore()
    up, down = (y + 1) % 4, (y + 3) % 4
    for k in range(1, 8):
        pl.semaphore_signal(barrier, inc=1, device_id=at_z((z + k) % 8), device_id_type=MESH)
        pl.semaphore_signal(barrier, inc=1, device_id={"mkt": (mkt + k) % 8}, device_id_type=MESH)
    pl.semaphore_signal(barrier, inc=1, device_id=at_y(up), device_id_type=MESH)
    pl.semaphore_signal(barrier, inc=1, device_id=at_y(down), device_id_type=MESH)

    def offset(j):
        return jnp.clip(QSTEP * (part * blocks + j) - (WIN - QSTEP) // 2, 0, quote_count - WIN) - base

    loads[0].wait()
    loads[1].wait()
    build(slab, kernel, offset, built)
    for h in range(2):
        landed[h, pl.ds(part * blocks, blocks)] = built[h, scen]
    pl.semaphore_wait(barrier, 16)

    def copy(src, dst, send, receive, device):
        return pltpu.make_async_remote_copy(
            src_ref=src, dst_ref=dst, send_sem=send, recv_sem=receive, device_id=device, device_id_type=MESH
        )

    sends = []

    def send(*args):
        c = copy(*args)
        c.start()
        sends.append(c)

    def piece(h, p):
        return landed.at[h, pl.ds(p * blocks, blocks)]

    def widen(h, p):
        at = pl.ds(p * blocks, blocks)
        table[h, at] = landed[h, at].astype(jnp.float32)

    def await_piece(h, p):
        copy(piece(h, p), piece(h, p), y_send.at[h, 0], recv.at[h, p], at_y(up)).wait_recv()
        widen(h, p)

    def arrival(k):
        return (z + 8 - (0, *ORDER)[k]) % 8

    def first_hop(h, k, start=True):
        p = y * 8 + arrival(k)
        hops = [
            copy(piece(h, p), piece(h, p), y_send.at[h, 3 * k + i], recv.at[h, p], at_y(to))
            for i, to in enumerate((up, down))
        ]
        for hop in hops:
            if start:
                hop.start()
            else:
                hop.wait_send()

    def second_hop(h, k, start=True):
        source = arrival(k)
        even = source % 2 == 0
        near, far = jnp.where(even, down, up), jnp.where(even, up, down)
        p = near * 8 + source
        hop = copy(piece(h, p), piece(h, p), y_send.at[h, 3 * k + 2], recv.at[h, p], at_y(far))
        if start:
            await_piece(h, p)
            hop.start()
        else:
            hop.wait_send()

    def rest(h, k):
        source = arrival(k)
        await_piece(h, jnp.where(source % 2 == 0, up, down) * 8 + source)
        await_piece(h, (y + 2) % 4 * 8 + source)

    for h in range(2):
        for k, d in enumerate(ORDER):
            to = (z + d) % 8
            send(built.at[h, to % 4], piece(h, part), z_send.at[h, k], recv.at[h, part], at_z(to))

    for k in range(8):
        if k:
            await_piece(0, y * 8 + arrival(k))
        first_hop(0, k)
        if k == 0:
            widen(0, part)
            widen(1, part)
            for load in loads[2:]:
                load.wait()
            prepare(w_in, w_mid, b_mid, w_out, embed, e32, w1, w2t, b2, w3)
            prepare_reduce(rank, position, span, weight_sum, picked, spread)
        if k >= LAG:
            second_hop(0, k - LAG)
    for k in range(8 - LAG, 8):
        second_hop(0, k)
    for k in range(8):
        if k:
            await_piece(1, y * 8 + arrival(k))
        first_hop(1, k)
    for k in range(8):
        rest(0, k)

    def beside(step):
        for pair in range(4):
            @pl.when(step == pair)
            def _():
                second_hop(1, 2 * pair)
                second_hop(1, 2 * pair + 1)

    price(0, idx, table.at[0], e32, w1, w2t, b2, w3, h1, h2, values, beside)
    for k in range(8):
        rest(1, k)
    price(1, idx, table.at[1], e32, w1, w2t, b2, w3, h1, h2, values)
    reduce_values(values, picked, spread, msg, pnl)

    got_mkt[mkt] = msg[...]
    got_pnl[trade] = pnl[...]
    for k in range(1, 8):
        send(msg, got_mkt.at[mkt], t_send.at[k - 1], r_mkt.at[mkt], {"mkt": (mkt + k) % 8})
    for k in range(1, 8):
        send(pnl, got_pnl.at[trade], t_send.at[6 + k], r_pnl.at[trade], {"trade": (trade + k) % 8})
    for k in range(1, 8):
        other = (mkt + k) % 8
        copy(msg, got_mkt.at[other], t_send.at[0], r_mkt.at[other], {"mkt": other}).wait_recv()
    total = got_mkt[0]
    for k in range(1, 8):
        total = total + got_mkt[k]
    got_marg[scen] = total[:16]
    got_short[part] = total[16:17]
    for k in range(1, 32):
        other = (part + k) % 32
        send(
            got_short.at[part], got_short.at[part], t_send.at[16 + k], r_short.at[part],
            {"trade": other // 4, "scen": other % 4},
        )
    for k in range(1, 4):
        send(got_marg.at[scen], got_marg.at[scen], t_send.at[13 + k], r_marg.at[scen], {"scen": (scen + k) % 4})
    for k in range(1, 8):
        other = (trade + k) % 8
        copy(pnl, got_pnl.at[other], t_send.at[0], r_pnl.at[other], {"trade": other}).wait_recv()
    total = got_pnl[0]
    for k in range(1, 8):
        total = total + got_pnl[k]
    pnl_out[...] = total[0, :16]
    for k in range(1, 4):
        other = (scen + k) % 4
        copy(got_marg.at[other], got_marg.at[other], t_send.at[0], r_marg.at[other], {"scen": other}).wait_recv()
    marg_out[...] = ((got_marg[0] + got_marg[1]) + (got_marg[2] + got_marg[3])).reshape(-1)
    for k in range(1, 32):
        other = (part + k) % 32
        copy(
            got_short.at[other], got_short.at[other], t_send.at[0], r_short.at[other], {"scen": scen}
        ).wait_recv()
    total = got_short[0]
    for k in range(1, 32):
        total = total + got_short[k]
    short_out[...] = total[0, :1]
    for c in sends:
        c.wait_send()
    for h in range(2):
        for k in range(8):
            first_hop(h, k, start=False)
            second_hop(h, k, start=False)


def local(quotes, kernel, trade_block, trade_embed, position, scen_rank, w_in, w_mid, b_mid, w_out):
    rows, quote_count = quotes.shape
    blocks = kernel.shape[0]
    scen_total = scen_rank.shape[0] * lax.axis_size("mkt") * lax.axis_size("scen")
    span = scen_total // 20
    weight_sum = math.fsum(math.exp(-r / span) for r in range(scen_total))
    trades, hid = trade_embed.shape
    groups = trades // 16
    slots = 2 * UNROLL
    vmem = pl.BlockSpec(memory_space=pltpu.VMEM)
    hbm = pl.BlockSpec(memory_space=pl.ANY)
    bf16, f32 = jnp.bfloat16, jnp.float32
    dma = pltpu.SemaphoreType.DMA
    marg, pnl, short = pl.pallas_call(
        functools.partial(fused_kernel, span, weight_sum, quote_count),
        out_shape=(
            jax.ShapeDtypeStruct((trades,), f32),
            jax.ShapeDtypeStruct((16,), f32),
            jax.ShapeDtypeStruct((1,), f32),
        ),
        in_specs=[hbm] * 10,
        out_specs=(vmem, vmem, vmem),
        scratch_shapes=[
            pltpu.VMEM((rows, SLAB), bf16),
            pltpu.VMEM(kernel.shape, bf16),
            pltpu.VMEM(trade_embed.shape, bf16),
            pltpu.SMEM(trade_block.shape, jnp.int32),
            pltpu.SMEM(scen_rank.shape, jnp.int32),
            pltpu.VMEM((16, groups), f32),
            pltpu.VMEM(w_in.shape, bf16),
            pltpu.VMEM(w_mid.shape, bf16),
            pltpu.VMEM(b_mid.shape, f32),
            pltpu.VMEM(w_out.shape, bf16),
            pltpu.VMEM((groups, 256), f32),
            pltpu.VMEM((24, 256), f32),
            pltpu.VMEM((2, rows // 16, blocks, 8, SEG), bf16),
            pltpu.VMEM((2, 32 * blocks, 8, SEG), bf16),
            pltpu.VMEM((2, 32 * blocks, 8, SEG), f32),
            pltpu.VMEM((2, trades, 128), f32),
            pltpu.VMEM((SEG, hid), bf16),
            pltpu.VMEM((hid, hid), bf16),
            pltpu.VMEM((hid, 256), f32),
            pltpu.VMEM((16, hid), bf16),
            pltpu.VMEM((slots, 256, hid), bf16),
            pltpu.VMEM((slots, hid, 256), bf16),
            pltpu.VMEM((2, groups, 128), f32),
            pltpu.VMEM((24, groups), f32),
            pltpu.VMEM((1, 128), f32),
            pltpu.VMEM((8, 24, groups), f32),
            pltpu.VMEM((8, 1, 128), f32),
            pltpu.VMEM((4, 16, groups), f32),
            pltpu.VMEM((32, 1, 128), f32),
            dma((10,)), dma((2, 7)), dma((2, 24)), dma((2, 32)), dma((48,)), dma((8,)), dma((8,)), dma((4,)), dma((32,)),
        ],
        compiler_params=pltpu.CompilerParams(
            vmem_limit_bytes=40 << 20, collective_id=0, has_side_effects=True
        ),
        name="shortfall",
    )(
        *(
            pltpu.with_memory_space_constraint(a, pltpu.HBM)
            for a in (
                quotes, kernel, trade_embed, trade_block, scen_rank, position.reshape(16, groups),
                w_in, w_mid, b_mid, w_out,
            )
        )
    )
    return (pnl, marg, short[0])


def solution(mesh):
    placed = (
        P("mkt", None),
        P(("trade", "scen"), None, None),
        P("trade"),
        P("trade", None),
        P("trade"),
        P(("mkt", "scen")),
        P(),
        P(),
        P(),
        P(),
    )
    return jax.shard_map(
        local,
        mesh=mesh,
        in_specs=placed,
        out_specs=(P(("mkt", "scen")), P("trade"), P()),
        check_vma=False,
    )
```

time: 87.2 us -> 60.6 us (0.69)
  Pallas kernels: 76.7 us -> 57 us
  local copies, waits for them, and re-layouts: 9.39 us -> 1.11 us
  between operations: 0.67 us -> 2.33 us
    pallas_call x1, Pallas kernels: 76.7 us -> 57 us  [local(): pl.pallas_call(functools.partial(fused_kernel, span, weight_sum, quote_co...]
    unnamed x21 -> x2, local copies, waits for them, and re-layouts: 8.36 us -> 1.11 us
where the time goes in v3:
time: 60.6 us; the launch traced here: 60.5 us
  Pallas kernels  57 us (94%)
  between operations  2.33 us (4%)
  local copies, waits for them, and re-layouts  1.11 us (2%)
    pallas_call x1, Pallas kernels, local(): pl.pallas_call(functools.partial(fused_kernel, span, weight_sum, quote_co...  57 us

profile of v3, /device:TPU:1, one launch (start us, length us, event | category | flops | bytes accessed | tf_op | source)
XLA Modules:
  0.0 60.5 jit_solution(15907200371131562892)
XLA Ops:
  0.6 57.0 %shortfall.1 = (f32[2048]{0:T(1024)S(1)}, f32[16]{0:T(128)S(1)}, f32[1]{0:T(128)}) custom-call(bf16[64,4096]{1,0:T(8,128)(2,1)} %quotes_hbm.1, bf16[16,128,128]{2,1,0:T(8,128)(2,1)} %kernel_hbm.1, bf16[2048,256]{1,0:T(8,128)(2,1)} %embed_hbm.1, s32[2048]{0:T(1024)} %idx_hbm.1, s32[16]{0:T(128)} %rank_hbm.1, f32[16,128]{1,0:T(8,128)} %bitcast.2, ...), custom_call_target="tpu_custom_call" | custom-call | tf_op jit(solution)/shard_map/shortfall/pallas_call | solution.py:340
  57.7 0.5 copy.16
  58.2 0.6 copy.17

commit v4 on v3

--- a/solution.py
+++ b/solution.py
@@ -12,8 +12,27 @@
 WIN = 128
 QSTEP = 8
 SLAB = 384
-LAG = 3
 ORDER = (1, 7, 2, 6, 4, 3, 5)
+DIRECT = frozenset([(0, 0), (0, 1), (0, 2), (0, 3), (0, 4), (0, 5), (0, 6), (0, 7), (1, 0), (1, 1), (1, 2), (1, 3), (1, 4), (1, 5), (1, 6), (1, 7)])
+EXCHANGE = (
+    (0, 1, 0),
+    (0, 1, 1),
+    (0, 1, 2),
+    (0, 1, 3),
+    (0, 1, 4),
+    (0, 1, 5),
+    (0, 1, 6),
+    (0, 1, 7),
+    (1, 1, 0),
+    (1, 1, 1),
+    (1, 1, 2),
+    (1, 1, 3),
+    (1, 1, 4),
+    (1, 1, 5),
+    (1, 1, 6),
+    (1, 1, 7),
+)
+LATER = ()
 HIGHEST = lax.Precision.HIGHEST
 MESH = pl.DeviceIdType.MESH
 UNROLL = 4
@@ -33,16 +52,17 @@
         e32[1, pl.ds(r, 64), :] = t[:, 128:]
 
 
-def price(half, idx, table, e32, w1, w2t, b2, w3, h1, h2, values, beside=lambda k: None):
+def price(idx, table, e32, w1, w2t, b2, w3, h1, h2, values, beside, between):
     groups = values.shape[1] // 2
     u_count = UNROLL
     trades = [(c, j) for c in range(2) for j in range(16)]
+    chunks = groups // u_count
 
     def row(g, c, j):
         return j * 2 * groups + c * groups + g
 
-    def first(g, slot):
-        x = jnp.concatenate([table[idx[row(g, c, j)]] for c, j in trades], axis=0).astype(jnp.bfloat16)
+    def first(half, g, slot):
+        x = jnp.concatenate([table[half, idx[row(g, c, j)]] for c, j in trades], axis=0).astype(jnp.bfloat16)
         e = jnp.concatenate(
             [
                 jnp.concatenate([e32.at[i][pl.ds(row(g, c, j), 8, stride=0), :] for c, j in trades], axis=0)
@@ -58,28 +78,39 @@
         z = z + b2[...]
         h2[slot] = (z + z * jnp.tanh(z)).astype(jnp.bfloat16)
 
-    def third(g, slot):
+    def third(half, g, slot):
         v = jnp.dot(w3[...], h2[slot], preferred_element_type=jnp.float32)
         values[half, pl.ds(g, 1), :] = v[0:1, :128]
         values[half, pl.ds(g + groups, 1), :] = v[0:1, 128:]
 
-    def step(i, a, b):
+    def step(parity, last, middle, ahead):
+        a, b = parity * u_count, (1 - parity) * u_count
         for u in range(u_count):
-            first(jnp.minimum((i + 2) * u_count + u, groups - 1), a + u)
-            second(b + u)
-            third(i * u_count + u, a + u)
+            if ahead is not None:
+                first(ahead[0], ahead[1] * u_count + u, a + u)
+            if middle:
+                second(b + u)
+            third(last[0], last[1] * u_count + u, a + u)
 
     for u in range(u_count):
-        first(u, u)
+        first(0, u, u)
     for u in range(u_count):
         second(u)
-        first(u_count + u, u_count + u)
-
-    @pl.loop(0, groups // u_count // 2)
-    def _(k):
-        beside(k)
-        step(2 * k, 0, u_count)
-        step(2 * k + 1, u_count, 0)
+        first(0, u_count + u, u_count + u)
+
+    for half in range(2):
+        @pl.loop(0, chunks // 2 - 1)
+        def _(k):
+            if half == 0:
+                beside(k)
+            step(0, (half, 2 * k), True, (half, 2 * k + 2))
+            step(1, (half, 2 * k + 1), True, (half, 2 * k + 3))
+
+        if half == 0:
+            between()
+        ahead = ((1, 0), (1, 1)) if half == 0 else (None, None)
+        step(0, (half, chunks - 2), True, ahead[0])
+        step(1, (half, chunks - 1), half == 0, ahead[1])
 
 
 def prepare_reduce(rank, position, span, weight_sum, picked, spread):
@@ -98,15 +129,12 @@
     )
 
 
-def reduce_values(values, picked, spread, marg, pnl):
+def reduce_trades(values, picked, spread, pnl, short):
     width = picked.shape[1]
-    groups = values.shape[1]
-    v = jnp.concatenate([values[0], values[1]], axis=1)
-    marg[0:16] = -lax.dot_general(
-        picked[0:16], v, (((1,), (1,)), ((), ())), precision=HIGHEST, preferred_element_type=jnp.float32
-    )
-    held = jnp.sum(v * spread[...], axis=0, keepdims=True)
-    marg[16:24] = jnp.broadcast_to(-jnp.sum(held * picked[16:17], axis=1, keepdims=True), (8, groups))
+    held = jnp.concatenate(
+        [jnp.sum(values[h] * spread[:, 128 * h : 128 * h + 128], axis=0, keepdims=True) for h in range(2)], axis=1
+    )
+    short[...] = jnp.broadcast_to(-jnp.sum(held * picked[16:17], axis=1, keepdims=True), short.shape)
     lane = lax.broadcasted_iota(jnp.int32, (width, 128), 0)
     fold = lane // 128 * 8 + lane % 8 == lax.broadcasted_iota(jnp.int32, (width, 128), 1)
     pnl[...] = jnp.dot(
@@ -115,12 +143,22 @@
     )[0:1]
 
 
-def build(slab, kernel, offset, built):
+def reduce_scenarios(values, picked, marg):
+    v = jnp.concatenate([values[0], values[1]], axis=1)
+    marg[...] = -lax.dot_general(
+        picked[0:16], v, (((1,), (1,)), ((), ())), precision=HIGHEST, preferred_element_type=jnp.float32
+    )
+
+
+def select(offset, picks):
+    apart = lax.broadcasted_iota(jnp.int32, (SLAB, WIN), 0) - lax.broadcasted_iota(jnp.int32, (SLAB, WIN), 1)
+    for j in range(picks.shape[0]):
+        picks[j] = jnp.where(apart == offset(j), 1.0, 0.0).astype(jnp.bfloat16)
+
+
+def build(slab, kernel, picks, built):
     for j in range(kernel.shape[0]):
-        pick = lax.broadcasted_iota(jnp.int32, (SLAB, WIN), 0) == lax.broadcasted_iota(jnp.int32, (SLAB, WIN), 1) + offset(j)
-        window = jnp.dot(
-            slab[...], jnp.where(pick, 1.0, 0.0).astype(jnp.bfloat16), preferred_element_type=jnp.float32
-        ).astype(jnp.bfloat16)
+        window = jnp.dot(slab[...], picks[j], preferred_element_type=jnp.float32).astype(jnp.bfloat16)
         state = jnp.dot(window, kernel[j], preferred_element_type=jnp.float32)
         for r in range(slab.shape[0] // 8):
             built[r % 2, r // 2, j] = state[8 * r : 8 * r + 8].astype(jnp.bfloat16)
@@ -130,8 +168,8 @@
     span, weight_sum, quote_count,
     quotes_hbm, kernel_hbm, embed_hbm, idx_hbm, rank_hbm, position_hbm, w_in_hbm, w_mid_hbm, b_mid_hbm, w_out_hbm,
     marg_out, pnl_out, short_out,
-    slab, kernel, embed, idx, rank, position, w_in, w_mid, b_mid, w_out, spread, picked, built, landed, table, e32, w1, w2t, b2, w3, h1, h2, values, msg, pnl,
-    got_mkt, got_pnl, got_marg, got_short, load_sem, z_send, y_send, recv, t_send, r_mkt, r_pnl, r_marg, r_short,
+    slab, picks, kernel, embed, idx, rank, position, w_in, w_mid, b_mid, w_out, spread, picked, built, landed, table, e32, w1, w2t, b2, w3, h1, h2, values, msg, pnl, short,
+    got_mkt, got_sum, got_pnl, got_marg, got_short, load_sem, z_send, y_send, recv, t_send, r_mkt, r_sum, r_pnl, r_marg, r_short,
 ):
     mkt, trade, scen = lax.axis_index("mkt"), lax.axis_index("trade"), lax.axis_index("scen")
     y, z_hi = trade // 2, trade % 2
@@ -166,18 +204,19 @@
     for k in range(1, 8):
         pl.semaphore_signal(barrier, inc=1, device_id=at_z((z + k) % 8), device_id_type=MESH)
         pl.semaphore_signal(barrier, inc=1, device_id={"mkt": (mkt + k) % 8}, device_id_type=MESH)
-    pl.semaphore_signal(barrier, inc=1, device_id=at_y(up), device_id_type=MESH)
-    pl.semaphore_signal(barrier, inc=1, device_id=at_y(down), device_id_type=MESH)
+    for k in range(1, 4):
+        pl.semaphore_signal(barrier, inc=1, device_id=at_y((y + k) % 4), device_id_type=MESH)
 
     def offset(j):
         return jnp.clip(QSTEP * (part * blocks + j) - (WIN - QSTEP) // 2, 0, quote_count - WIN) - base
 
+    select(offset, picks)
     loads[0].wait()
     loads[1].wait()
-    build(slab, kernel, offset, built)
+    build(slab, kernel, picks, built)
     for h in range(2):
         landed[h, pl.ds(part * blocks, blocks)] = built[h, scen]
-    pl.semaphore_wait(barrier, 16)
+    pl.semaphore_wait(barrier, 17)
 
     def copy(src, dst, send, receive, device):
         return pltpu.make_async_remote_copy(
@@ -209,7 +248,7 @@
         p = y * 8 + arrival(k)
         hops = [
             copy(piece(h, p), piece(h, p), y_send.at[h, 3 * k + i], recv.at[h, p], at_y(to))
-            for i, to in enumerate((up, down))
+            for i, to in enumerate((up, down, (y + 2) % 4) if (h, k) in DIRECT else (up, down))
         ]
         for hop in hops:
             if start:
@@ -218,6 +257,8 @@
                 hop.wait_send()
 
     def second_hop(h, k, start=True):
+        if (h, k) in DIRECT:
+            return
         source = arrival(k)
         even = source % 2 == 0
         near, far = jnp.where(even, down, up), jnp.where(even, up, down)
@@ -232,6 +273,8 @@
     def rest(h, k):
         source = arrival(k)
         await_piece(h, jnp.where(source % 2 == 0, up, down) * 8 + source)
+        if (h, k) in DIRECT:
+            await_piece(h, jnp.where(source % 2 == 0, down, up) * 8 + source)
         await_piece(h, (y + 2) % 4 * 8 + source)
 
     for h in range(2):
@@ -239,61 +282,66 @@
             to = (z + d) % 8
             send(built.at[h, to % 4], piece(h, part), z_send.at[h, k], recv.at[h, part], at_z(to))
 
-    for k in range(8):
-        if k:
-            await_piece(0, y * 8 + arrival(k))
-        first_hop(0, k)
-        if k == 0:
-            widen(0, part)
-            widen(1, part)
-            for load in loads[2:]:
-                load.wait()
-            prepare(w_in, w_mid, b_mid, w_out, embed, e32, w1, w2t, b2, w3)
-            prepare_reduce(rank, position, span, weight_sum, picked, spread)
-        if k >= LAG:
-            second_hop(0, k - LAG)
-    for k in range(8 - LAG, 8):
-        second_hop(0, k)
-    for k in range(8):
-        if k:
-            await_piece(1, y * 8 + arrival(k))
-        first_hop(1, k)
+    widen(0, part)
+    widen(1, part)
+    for h, hop, k in EXCHANGE:
+        if hop == 2:
+            second_hop(h, k)
+        else:
+            if k:
+                await_piece(h, y * 8 + arrival(k))
+            first_hop(h, k)
+            if h == 0 and k == 0:
+                for load in loads[2:]:
+                    load.wait()
+                prepare(w_in, w_mid, b_mid, w_out, embed, e32, w1, w2t, b2, w3)
+                prepare_reduce(rank, position, span, weight_sum, picked, spread)
     for k in range(8):
         rest(0, k)
 
     def beside(step):
-        for pair in range(4):
-            @pl.when(step == pair)
+        for at, hops in enumerate(LATER):
+            @pl.when(step == at)
             def _():
-                second_hop(1, 2 * pair)
-                second_hop(1, 2 * pair + 1)
-
-    price(0, idx, table.at[0], e32, w1, w2t, b2, w3, h1, h2, values, beside)
-    for k in range(8):
-        rest(1, k)
-    price(1, idx, table.at[1], e32, w1, w2t, b2, w3, h1, h2, values)
-    reduce_values(values, picked, spread, msg, pnl)
-
+                for k in hops:
+                    second_hop(1, k)
+
+    def between():
+        for k in range(8):
+            rest(1, k)
+
+    price(idx, table, e32, w1, w2t, b2, w3, h1, h2, values, beside, between)
+    reduce_trades(values, picked, spread, pnl, short)
+    got_sum[mkt] = short[...]
+    got_pnl[trade] = pnl[...]
+    for k in range(1, 8):
+        send(short, got_sum.at[mkt], t_send.at[47 + k], r_sum.at[mkt], {"mkt": (mkt + k) % 8})
+    for k in range(1, 8):
+        send(pnl, got_pnl.at[trade], t_send.at[6 + k], r_pnl.at[trade], {"trade": (trade + k) % 8})
+    reduce_scenarios(values, picked, msg)
     got_mkt[mkt] = msg[...]
-    got_pnl[trade] = pnl[...]
     for k in range(1, 8):
         send(msg, got_mkt.at[mkt], t_send.at[k - 1], r_mkt.at[mkt], {"mkt": (mkt + k) % 8})
     for k in range(1, 8):
-        send(pnl, got_pnl.at[trade], t_send.at[6 + k], r_pnl.at[trade], {"trade": (trade + k) % 8})
-    for k in range(1, 8):
         other = (mkt + k) % 8
-        copy(msg, got_mkt.at[other], t_send.at[0], r_mkt.at[other], {"mkt": other}).wait_recv()
-    total = got_mkt[0]
-    for k in range(1, 8):
-        total = total + got_mkt[k]
-    got_marg[scen] = total[:16]
-    got_short[part] = total[16:17]
+        copy(short, got_sum.at[other], t_send.at[0], r_sum.at[other], {"mkt": other}).wait_recv()
+    total = got_sum[0]
+    for k in range(1, 8):
+        total = total + got_sum[k]
+    got_short[part] = total
     for k in range(1, 32):
         other = (part + k) % 32
         send(
             got_short.at[part], got_short.at[part], t_send.at[16 + k], r_short.at[part],
             {"trade": other // 4, "scen": other % 4},
         )
+    for k in range(1, 8):
+        other = (mkt + k) % 8
+        copy(msg, got_mkt.at[other], t_send.at[0], r_mkt.at[other], {"mkt": other}).wait_recv()
+    total = got_mkt[0]
+    for k in range(1, 8):
+        total = total + got_mkt[k]
+    got_marg[scen] = total
     for k in range(1, 4):
         send(got_marg.at[scen], got_marg.at[scen], t_send.at[13 + k], r_marg.at[scen], {"scen": (scen + k) % 4})
     for k in range(1, 8):
@@ -322,6 +370,12 @@
         for k in range(8):
             first_hop(h, k, start=False)
             second_hop(h, k, start=False)
+
+
+def hand_on(marg, pnl, short, marg_out, pnl_out, short_out):
+    marg_out[...] = marg[...]
+    pnl_out[...] = pnl[...]
+    short_out[...] = short[...]
 
 
 def local(quotes, kernel, trade_block, trade_embed, position, scen_rank, w_in, w_mid, b_mid, w_out):
@@ -348,6 +402,7 @@
         out_specs=(vmem, vmem, vmem),
         scratch_shapes=[
             pltpu.VMEM((rows, SLAB), bf16),
+            pltpu.VMEM((blocks, SLAB, WIN), bf16),
             pltpu.VMEM(kernel.shape, bf16),
             pltpu.VMEM(trade_embed.shape, bf16),
             pltpu.SMEM(trade_block.shape, jnp.int32),
@@ -370,13 +425,15 @@
             pltpu.VMEM((slots, 256, hid), bf16),
             pltpu.VMEM((slots, hid, 256), bf16),
             pltpu.VMEM((2, groups, 128), f32),
-            pltpu.VMEM((24, groups), f32),
+            pltpu.VMEM((16, groups), f32),
             pltpu.VMEM((1, 128), f32),
-            pltpu.VMEM((8, 24, groups), f32),
+            pltpu.VMEM((1, 128), f32),
+            pltpu.VMEM((8, 16, groups), f32),
+            pltpu.VMEM((8, 1, 128), f32),
             pltpu.VMEM((8, 1, 128), f32),
             pltpu.VMEM((4, 16, groups), f32),
             pltpu.VMEM((32, 1, 128), f32),
-            dma((10,)), dma((2, 7)), dma((2, 24)), dma((2, 32)), dma((48,)), dma((8,)), dma((8,)), dma((4,)), dma((32,)),
+            dma((10,)), dma((2, 7)), dma((2, 24)), dma((2, 32)), dma((56,)), dma((8,)), dma((8,)), dma((8,)), dma((4,)), dma((32,)),
         ],
         compiler_params=pltpu.CompilerParams(
             vmem_limit_bytes=40 << 20, collective_id=0, has_side_effects=True
@@ -391,6 +448,14 @@
             )
         )
     )
+    marg, pnl, short = pl.pallas_call(
+        hand_on,
+        out_shape=tuple(jax.ShapeDtypeStruct(a.shape, f32) for a in (marg, pnl, short)),
+        in_specs=[vmem] * 3,
+        out_specs=(vmem,) * 3,
+        compiler_params=pltpu.CompilerParams(vmem_limit_bytes=1 << 20),
+        name="results",
+    )(marg, pnl, short)
     return (pnl, marg, short[0])
 
 

time: 60.6 us -> 57.7 us (0.952)
  between operations: 2.33 us -> 0.64 us
  local copies, waits for them, and re-layouts: 1.11 us -> 0 us
    pallas_call x1, Pallas kernels: 57 us -> 55.7 us  [local(): pl.pallas_call(functools.partial(fused_kernel, span, weight_sum, quote_co...]
    pallas_call x0 -> x1, Pallas kernels: none -> 1.24 us  [local(): pl.pallas_call(hand_on, out_shape=tuple((jax.ShapeDtypeStruct(a.shape, f3...]
    unnamed x2 -> x0, local copies, waits for them, and re-layouts: 1.11 us -> none
where the time goes in v4:
time: 57.7 us; the launch traced here: 57.6 us
  Pallas kernels  57 us (99%)
  between operations  0.64 us (1%)
    pallas_call x1, Pallas kernels, local(): pl.pallas_call(functools.partial(fused_kernel, span, weight_sum, quote_co...  55.7 us
    pallas_call x1, Pallas kernels, local(): pl.pallas_call(hand_on, out_shape=tuple((jax.ShapeDtypeStruct(a.shape, f3...  1.24 us

profile of v4, /device:TPU:1, one launch (start us, length us, event | category | flops | bytes accessed | tf_op | source)
XLA Modules:
  0.0 57.6 jit_solution(2606369753423674653)
XLA Ops:
  0.6 55.7 %shortfall.1 = (f32[2048]{0:T(1024)S(1)}, f32[16]{0:T(128)S(1)}, f32[1]{0:T(128)}) custom-call(bf16[64,4096]{1,0:T(8,128)(2,1)} %quotes_hbm.1, bf16[16,128,128]{2,1,0:T(8,128)(2,1)} %kernel_hbm.1, bf16[2048,256]{1,0:T(8,128)(2,1)} %embed_hbm.1, s32[2048]{0:T(1024)} %idx_hbm.1, s32[16]{0:T(128)} %rank_hbm.1, f32[16,128]{1,0:T(8,128)} %bitcast.2, ...), custom_call_target="tpu_custom_call" | custom-call | tf_op jit(solution)/shard_map/shortfall/pallas_call | solution.py:394
  56.4 1.2 %results.1 = (f32[2048]{0:T(1024)}, f32[16]{0:T(128)}, f32[1]{0:T(128)}) custom-call(f32[2048]{0:T(1024)S(1)} %get-tuple-element.9.marg, f32[16]{0:T(128)S(1)} %get-tuple-element.10.pnl, f32[1]{0:T(128)} %get-tuple-element.11.short), custom_call_target="tpu_custom_call" | custom-call | tf_op jit(solution)/shard_map/results/pallas_call | solution.py:451
